TPU v7x, 256 devices: a whole 4x4x8 slice. The times are simulated.
256 devices in a mesh: row: 32 (over z_lo, y, core), col: 8 (over x, z_hi).
Axes of the slice: x: 4, y: 4, z: 8 (z_hi: 2, z_lo: 4; z = z_hi * 4 + z_lo), core: 2. Of those that a mesh axis runs over, the one named last changes fastest.
Arguments:
- spectral_field: float32 [2, 256, 256, 256], P(None, 'row', 'col'), may hold values from -4.5 to 4.5
Outputs:
- updated_field: float32 [2, 256, 256, 256], P(None, 'row', 'col')
- shell_spectrum: float32 [256], replicated
All inputs are finite; a program needn't handle non-finite values.
Results may differ from a plain program's by a relative error of at most 0.0031.
Values may be sent and summed in bfloat16 or wider, within the bound.
No kernel may reach another device: no remote copies, remote signals or barrier semaphores. Data moves between devices by JAX's collectives and lax.ppermute only.
A program may use at most 64 MiB of HBM per device.

v0:
```python
import math

import jax
import jax.numpy as jnp
import numpy as np
from jax import lax
from jax.experimental import pallas as pl
from jax.experimental.pallas import tpu as pltpu
from jax.sharding import Mesh
from jax.sharding import PartitionSpec as P

ROW = ("z_lo", "y", "core")
COL = ("x", "z_hi")
RING = ("z_hi", "z_lo", "y", "x", "core")

phase_rate = 0.0002
coupling = 0.2

F32 = jnp.float32
BF16 = jnp.bfloat16


def trig(waves, points, length):
    turns = np.mod(np.asarray(waves)[:, None] * np.asarray(points)[None, :], length)
    angle = turns.astype(np.float32) * np.float32(2.0 * math.pi / length)
    return np.cos(angle).astype(np.float32), np.sin(angle).astype(np.float32)


def to_slabs(field_ref, table_ref, out_ref, wide_ref, *, scale):
    modes = field_ref.shape[3]
    width = field_ref.shape[2]
    lane = lax.broadcasted_iota(jnp.int32, (width, modes), 1)
    sign = jnp.where(lane % 2 == 0, 1.0, -1.0)
    table = table_ref[...]
    width_x = field_ref.shape[1]
    for pair in range(0, width_x, 2):
        rows = []
        for at in (pair, pair + 1):
            real, imag = field_ref[0, at], field_ref[1, at]
            for factor in (None, sign):
                if factor is not None:
                    real, imag = real * factor, imag * factor
                rows.append(jnp.concatenate([real, -imag], axis=1).astype(BF16))
                rows.append(jnp.concatenate([imag, real], axis=1).astype(BF16))
        block = jnp.concatenate(rows, axis=0)
        product = lax.dot_general(
            table, block, (((1,), (1,)), ((), ())), preferred_element_type=F32
        ) * scale
        for k in range(2):
            wide_ref[pl.ds(pair + k, modes, stride=width_x), :] = product[:, 128 * k : 128 * (k + 1)]
    out_ref[...] = wide_ref[...].astype(BF16).reshape(out_ref.shape)


def planes(in_ref, ty_ref, tx_ref, fx_ref, fy_ref, out_ref, back_ref, done_ref, *, scale_in, scale_out, chunk):
    modes = 256
    grid = 512
    half = 64
    for plane in range(2):
        parts = []
        for x in range(4):
            for z in range(2):
                block = in_ref[z, :, x].reshape(modes, 128)
                parts.append(block[:, half * plane : half * (plane + 1)])
        lines = jnp.concatenate(parts, axis=1)
        along_y = (jnp.dot(lines, ty_ref[...], preferred_element_type=F32) * scale_in).astype(BF16)
        first = lax.broadcasted_iota(jnp.int32, (modes, chunk), 0) == 0
        for start in range(0, grid, chunk):
            rhs = jnp.concatenate(
                [along_y[:, start : start + chunk], along_y[:, grid + start : grid + start + chunk]], axis=1
            )
            even_odd = jnp.dot(tx_ref[...], rhs, preferred_element_type=F32) * scale_in
            pr, pi = even_odd[:modes, :chunk], even_odd[:modes, chunk:]
            qr, qi = even_odd[modes:, :chunk], even_odd[modes:, chunk:]
            ar = jnp.where(first, pr, pr - qi)
            ai = jnp.where(first, pi, pi + qr)
            br = jnp.where(first, qr, pr + qi)
            bi = jnp.where(first, qi, pi - qr)
            ma = coupling * (ar * ar + ai * ai)
            mb = coupling * (br * br + bi * bi)
            ar, ai, br, bi = ma * ar, ma * ai, mb * br, mb * bi
            even_r = jnp.where(first, ar, ar + br)
            even_i = jnp.where(first, ai, ai + bi)
            odd_i = jnp.where(first, br, ai - bi)
            odd_r = jnp.where(first, bi, br - ar)
            folded = jnp.concatenate(
                [
                    jnp.concatenate([even_r.astype(BF16), even_i.astype(BF16)], axis=1),
                    jnp.concatenate([odd_i.astype(BF16), odd_r.astype(BF16)], axis=1),
                ],
                axis=0,
            )
            back_x = (jnp.dot(fx_ref[...], folded, preferred_element_type=F32) * scale_out).astype(BF16)
            back_ref[:, start : start + chunk] = back_x[:, :chunk]
            back_ref[:, grid + start : grid + start + chunk] = back_x[:, chunk:]
        done_ref[plane] = (
            jnp.dot(back_ref[...], fy_ref[...], preferred_element_type=F32) * scale_out
        ).astype(BF16)
    for x in range(4):
        for z in range(2):
            at = 128 * x + half * z
            message = jnp.concatenate([done_ref[0, :, at : at + half], done_ref[1, :, at : at + half]], axis=1)
            out_ref[z, :, x] = message.reshape(16, 16, 128)


def finish(in_ref, field_ref, table_ref, out_ref, sums_ref, wide_ref, energy_ref, *, scale, bins):
    _, width_x, width_y, modes = field_ref.shape
    half_modes = modes // 2
    row = (lax.axis_index("z_lo") * 4 + lax.axis_index("y")) * 2 + lax.axis_index("core")
    col = lax.axis_index("x") * 2 + lax.axis_index("z_hi")
    base_x = row * width_x - half_modes
    base_y = col * width_y - half_modes
    wave_y = base_y + lax.broadcasted_iota(jnp.int32, (width_y, modes), 0)
    wave_z = lax.broadcasted_iota(jnp.int32, (width_y, modes), 1) - half_modes
    square_yz = wave_y * wave_y + wave_z * wave_z
    angle_yz = phase_rate * square_yz.astype(F32)
    cos_yz, sin_yz = jnp.cos(angle_yz), jnp.sin(angle_yz)
    wave_x8 = base_x + lax.broadcasted_iota(jnp.int32, (width_x, modes), 0)
    angle_x = phase_rate * (wave_x8 * wave_x8).astype(F32)
    cos_x, sin_x = jnp.cos(angle_x), jnp.sin(angle_x)
    near_x = jnp.maximum(base_x, -(base_x + width_x - 1))
    near_y = jnp.maximum(base_y, -(base_y + width_y - 1))
    near = near_x * near_x + near_y * near_y

    def shell_of(squared):
        return jnp.floor(jnp.sqrt(squared.astype(F32)) + 0.5).astype(jnp.int32)

    lowest = shell_of(near + wave_z * wave_z)
    sign = jnp.where(wave_z % 2 == 0, 1.0, -1.0)
    wide_ref[...] = in_ref[...].reshape(wide_ref.shape).astype(F32)
    table = table_ref[...]
    for at in range(width_x):
        slab = wide_ref[pl.ds(at, modes, stride=width_x), :].astype(BF16)
        got = lax.dot_general(slab, table, (((0,), (0,)), ((), ())), preferred_element_type=F32)
        r0, i0, r1, i1 = (got[width_y * k : width_y * (k + 1)] for k in range(4))
        non_r = (r0[:, :modes] + i0[:, modes:] + sign * (r1[:, :modes] + i1[:, modes:])) * scale
        non_i = (i0[:, :modes] - r0[:, modes:] + sign * (i1[:, :modes] - r1[:, modes:])) * scale
        u = field_ref[0, at] - non_i
        v = field_ref[1, at] + non_r
        cx, sx = cos_x[at : at + 1], sin_x[at : at + 1]
        cos = cos_yz * cx - sin_yz * sx
        sin = sin_yz * cx + cos_yz * sx
        new_r = u * cos + v * sin
        new_i = v * cos - u * sin
        out_ref[0, at] = new_r
        out_ref[1, at] = new_i
        energy_ref[0, at] = new_r * new_r + new_i * new_i
        wx = base_x + at
        energy_ref[1, at] = (shell_of(square_yz + wx * wx) - lowest).astype(F32)
    rows = []
    for k in range(bins):
        total = jnp.zeros((8, modes), F32)
        for at in range(width_x):
            hit = jnp.where(energy_ref[1, at] == float(k), energy_ref[0, at], 0.0)
            for j in range(0, width_y, 8):
                total = total + hit[j : j + 8]
        rows.append(jnp.sum(total, axis=0, keepdims=True))
    stacked = jnp.concatenate(rows, axis=0)
    wave_col = lax.broadcasted_iota(jnp.int32, (modes, modes), 0) - half_modes
    shell_col = shell_of(near + wave_col * wave_col)
    one_hot = (shell_col == lax.broadcasted_iota(jnp.int32, (modes, modes), 1)).astype(F32)
    placed = jnp.dot(stacked, one_hot, preferred_element_type=F32, precision=lax.Precision.HIGHEST)
    shifted = pltpu.roll(placed, 0, 1, stride=1, stride_axis=0)
    sums_ref[...] = jnp.sum(shifted, axis=0, keepdims=True)


def tables(modes):
    grid = 2 * modes
    waves = np.arange(modes) - modes // 2
    cos, sin = trig(waves, np.arange(grid), grid)
    low_cos, low_sin = cos[:, :modes].T, sin[:, :modes].T
    z_table = np.concatenate([low_cos, low_sin], axis=1)
    blocks = modes // 32
    c, s = cos.reshape(blocks, 32, grid), sin.reshape(blocks, 32, grid)
    ty = np.stack([np.concatenate([c, s], 2), np.concatenate([-s, c], 2)], 1).reshape(2 * modes, 2 * grid)
    ct, st = c.transpose(2, 0, 1), s.transpose(2, 0, 1)
    fy = np.stack([np.stack([ct, -st], 2), np.stack([st, ct], 2)], 0).reshape(2 * grid, 2 * modes)
    odd = low_sin.copy()
    odd[0] = cos[:, modes]
    tx = np.concatenate([low_cos, odd], axis=0)
    fx = tx.T
    return [jnp.asarray(np.ascontiguousarray(t), BF16) for t in (z_table, ty, tx, fx, fy)]


def shell_counts(modes):
    wave = np.arange(modes) - modes // 2
    square = wave * wave
    total = square[:, None, None] + square[None, :, None] + square[None, None, :]
    shell = np.floor(np.sqrt(total.astype(np.float32)) + np.float32(0.5)).astype(np.int64)
    return np.bincount(shell.reshape(-1), minlength=modes)[:modes].astype(np.float32)


def params():
    return pltpu.CompilerParams(vmem_limit_bytes=48 * 1024 * 1024)


def body(field):
    _, width_x, width_y, modes = field.shape
    devices = lax.axis_size(RING)
    scale_in = 1.0 / math.sqrt(modes)
    scale_out = math.sqrt(modes) / (2 * modes)
    z_table, ty, tx, fx, fy = tables(modes)
    import functools

    messages = pl.pallas_call(
        functools.partial(to_slabs, scale=scale_in),
        out_shape=jax.ShapeDtypeStruct((devices, width_x, 128), BF16),
        scratch_shapes=[pltpu.VMEM((devices * width_x, 128), F32)],
        compiler_params=params(),
        name="to_slabs",
    )(field, z_table)
    slabs = lax.all_to_all(messages, RING, 0, 0, tiled=True)
    back = pl.pallas_call(
        functools.partial(planes, scale_in=scale_in, scale_out=scale_out, chunk=256),
        out_shape=jax.ShapeDtypeStruct((2, 16, 4, 16, 128), BF16),
        scratch_shapes=[pltpu.VMEM((modes, 4 * modes), BF16), pltpu.VMEM((2, modes, 2 * modes), BF16)],
        compiler_params=params(),
        name="planes",
    )(slabs.reshape(2, 16, 4, 16, 128), ty, tx, fx, fy)
    home = lax.all_to_all(back.reshape(devices, width_x, 128), RING, 0, 0, tiled=True)
    bins = 8 * math.ceil((math.sqrt((width_x - 1) ** 2 + (width_y - 1) ** 2) + 2) / 8)
    updated, sums = pl.pallas_call(
        functools.partial(finish, scale=scale_out, bins=bins),
        out_shape=[jax.ShapeDtypeStruct(field.shape, F32), jax.ShapeDtypeStruct((1, modes), F32)],
        scratch_shapes=[
            pltpu.VMEM((devices * width_x, 128), F32),
            pltpu.VMEM((2, width_x, width_y, modes), F32),
        ],
        compiler_params=params(),
        name="finish",
    )(home, field, z_table)
    copies = jnp.broadcast_to(sums.reshape(1, modes // 128, 128), (devices, modes // 128, 128))
    everyone = lax.all_to_all(copies, RING, 0, 0, tiled=True)
    spectrum = jnp.sum(everyone, axis=0).reshape(modes) / jnp.asarray(np.maximum(shell_counts(modes), 1.0))
    return updated, spectrum


def solution(mesh):
    split = Mesh(mesh.devices.reshape(4, 4, 2, 4, 2), ROW + COL)
    placed = (P(None, ROW, COL, None),)
    return jax.shard_map(
        body, mesh=split, in_specs=placed, out_specs=(P(None, ROW, COL, None), P()), check_vma=False
    )
```

profile of v0, /device:TPU:1, one launch (start us, length us, event | category | flops | bytes accessed | tf_op | source)
XLA Modules:
  0.0 94.3 jit_solution(8102516719549919469)
XLA Ops:
  0.6 0.0 copy-start
  0.6 1.0 %copy-done = f32[2,8,32,256]{3,2,1,0:T(8,128)S(1)} copy-done((f32[2,8,32,256]{3,2,1,0:T(8,128)S(1)}, f32[2,8,32,256]{3,2,1,0:T(8,128)}, u32[]{:S(2)}) %copy-start) | copy-done | bytes 524312
  1.7 0.0 copy-start.4
  1.7 0.9 %copy-done.4 = bf16[256,512]{1,0:T(8,128)(2,1)S(1)} copy-done((bf16[256,512]{1,0:T(8,128)(2,1)S(1)}, bf16[256,512]{1,0:T(8,128)(2,1)}, u32[]{:S(2)}) %copy-start.4) | copy-done | bytes 262168
  2.6 0.0 copy-start.2
  2.6 0.0 copy-start.3
  2.6 0.5 to_slabs.1
  3.2 0.0 copy-start.5
  3.2 35.3 %all_to_all.15 = bf16[256,8,128]{2,1,0:T(8,128)(2,1)S(1)} all-to-all(bf16[256,8,128]{2,1,0:T(8,128)(2,1)S(1)} %to_slabs.1), channel_id=1, replica_groups=mesh['z_lo'=4,'y'=4,'core'=2,'x'=4,'z_hi'=2] {'z_hi','z_lo','y','x','core'}, dimensions={0} | all-to-all | bytes 1048576 | tf_op jit(solution)/shard_map/all_to_all | solution.py:211
  38.5 0.0 copy-done.2
  38.5 0.0 copy-done.3
  38.5 0.0 copy-done.5
  38.5 0.0 copy-start.6
  38.5 0.9 copy-done.6
  39.5 3.9 %planes.1 = bf16[2,16,4,16,128]{4,3,2,1,0:T(8,128)(2,1)S(1)} custom-call(bf16[2,16,4,16,128]{4,3,2,1,0:T(8,128)(2,1)S(1)} %bitcast.5, bf16[512,1024]{1,0:T(8,128)(2,1)S(1)} %copy-done.3, bf16[512,256]{1,0:T(8,128)(2,1)S(1)} %copy-done.6, bf16[256,512]{1,0:T(8,128)(2,1)S(1)} %copy-done.5, bf16[1024,512]{1,0:T(8,128)(2,1)S(1)} %copy-done.2), custom_call_target="tpu_custom_call" | custom-call | tf_op jit(solution)/shard_map/planes/pallas_call | solution.py:212
  43.4 0.0 copy-start.1
  43.4 25.9 %all_to_all.16.in_ref = bf16[256,8,128]{2,1,0:T(8,128)(2,1)S(1)} all-to-all(bf16[256,8,128]{2,1,0:T(8,128)(2,1)S(1)} %bitcast.6), channel_id=1, replica_groups=mesh['z_lo'=4,'y'=4,'core'=2,'x'=4,'z_hi'=2] {'z_hi','z_lo','y','x','core'}, dimensions={0} | all-to-all | bytes 1048576 | tf_op jit(solution)/shard_map/all_to_all | solution.py:219
  69.3 0.0 copy-done.1
  69.3 2.4 %finish.1 = (f32[2,8,32,256]{3,2,1,0:T(8,128)}, f32[1,256]{1,0:T(1,128)S(1)}) custom-call(bf16[256,8,128]{2,1,0:T(8,128)(2,1)S(1)} %all_to_all.16.in_ref, f32[2,8,32,256]{3,2,1,0:T(8,128)S(1)} %copy-done.1, bf16[256,512]{1,0:T(8,128)(2,1)S(1)} %copy-done.4), custom_call_target="tpu_custom_call" | custom-call | tf_op jit(solution)/shard_map/finish/pallas_call | solution.py:221
  71.7 0.1 broadcast_in_dim.8
  71.8 21.2 %all_to_all.17 = f32[256,2,128]{2,1,0:T(2,128)S(1)} all-to-all(f32[256,2,128]{2,1,0:T(2,128)S(1)} %broadcast_in_dim.8), channel_id=1, replica_groups=mesh['z_lo'=4,'y'=4,'core'=2,'x'=4,'z_hi'=2] {'z_hi','z_lo','y','x','core'}, dimensions={0} | all-to-all | bytes 524288 | tf_op jit(solution)/shard_map/all_to_all | solution.py:232
  93.0 0.3 reduce_sum.9
  93.3 0.4 copy-done.7
  93.7 0.6 multiply_bitcast_fusion
  (1 shorter events, 0.0 us)
Async XLA Ops:
  0.6 1.0 %copy-start = (f32[2,8,32,256]{3,2,1,0:T(8,128)S(1)}, f32[2,8,32,256]{3,2,1,0:T(8,128)}, u32[]{:S(2)}) copy-start(f32[2,8,32,256]{3,2,1,0:T(8,128)} %field_ref.3) | copy-start | bytes 1572868
  1.7 0.9 %copy-start.4 = (bf16[256,512]{1,0:T(8,128)(2,1)S(1)}, bf16[256,512]{1,0:T(8,128)(2,1)}, u32[]{:S(2)}) copy-start(bf16[256,512]{1,0:T(8,128)(2,1)} %constant.14.clone.table_ref) | copy-start | bytes 786436
  2.6 35.9 %copy-start.2 = (bf16[1024,512]{1,0:T(8,128)(2,1)S(1)}, bf16[1024,512]{1,0:T(8,128)(2,1)}, u32[]{:S(2)}) copy-start(bf16[1024,512]{1,0:T(8,128)(2,1)} %constant.18.clone.fy_ref) | copy-start | bytes 3145732
  2.6 35.9 %copy-start.3 = (bf16[512,1024]{1,0:T(8,128)(2,1)S(1)}, bf16[512,1024]{1,0:T(8,128)(2,1)}, u32[]{:S(2)}) copy-start(bf16[512,1024]{1,0:T(8,128)(2,1)} %constant.15.clone.ty_ref) | copy-start | bytes 3145732
  3.2 35.4 %copy-start.5 = (bf16[256,512]{1,0:T(8,128)(2,1)S(1)}, bf16[256,512]{1,0:T(8,128)(2,1)}, u32[]{:S(2)}) copy-start(bf16[256,512]{1,0:T(8,128)(2,1)} %constant.17.clone.fx_ref) | copy-start | bytes 786436
  38.5 1.0 %copy-start.6 = (bf16[512,256]{1,0:T(8,128)(2,1)S(1)}, bf16[512,256]{1,0:T(8,128)(2,1)}, u32[]{:S(2)}) copy-start(bf16[512,256]{1,0:T(8,128)(2,1)} %constant.16.clone.tx_ref) | copy-start | bytes 786436
  43.4 25.9 %copy-start.1 = (f32[2,8,32,256]{3,2,1,0:T(8,128)S(1)}, f32[2,8,32,256]{3,2,1,0:T(8,128)}, u32[]{:S(2)}) copy-start(f32[2,8,32,256]{3,2,1,0:T(8,128)} %field_ref.3) | copy-start | bytes 1572868
  93.0 0.7 copy-start.7
where the time goes:
time: 94.6 us; the launch traced here: 94.3 us
  blocking collectives  82.5 us (87%)
  Pallas kernels  6.85 us (7%)
  local copies, waits for them, and re-layouts  3.42 us (4%)
    all_to_all x1, blocking collectives, body(): slabs = lax.all_to_all(messages, RING, 0, 0, tiled=True)  35.3 us
    all_to_all x1, blocking collectives, body(): lax.all_to_all(back.reshape(devices, width_x, 128), RING, 0, 0, tiled=True)  25.9 us
    all_to_all x1, blocking collectives, body(): everyone = lax.all_to_all(copies, RING, 0, 0, tiled=True)  21.2 us
    pallas_call x1, Pallas kernels, body(): pl.pallas_call(functools.partial(planes, scale_in=scale_in, scale_out=sca...  3.93 us
    unnamed x16, local copies, waits for them, and re-layouts  3.35 us
    pallas_call x1, Pallas kernels, body(): pl.pallas_call(functools.partial(finish, scale=scale_out, bins=bins), out...  2.39 us

commit v1 on v0

--- a/solution.py
+++ b/solution.py
@@ -1,3 +1,4 @@
+import functools
 import math
 
 import jax
@@ -26,17 +27,24 @@
     return np.cos(angle).astype(np.float32), np.sin(angle).astype(np.float32)
 
 
-def to_slabs(field_ref, table_ref, out_ref, wide_ref, *, scale):
-    modes = field_ref.shape[3]
-    width = field_ref.shape[2]
+def to_slabs(field_ref, table_hbm, out_ref, wide_ref, field, table, field_sems, table_sem, *, scale):
+    _, width_x, width, modes = field_ref.shape
+    table_copy = pltpu.make_async_copy(table_hbm, table, table_sem)
+    copies = [
+        pltpu.make_async_copy(field_ref.at[:, pl.ds(at, 2)], field.at[:, pl.ds(at, 2)], field_sems.at[at // 2])
+        for at in range(0, width_x, 2)
+    ]
+    table_copy.start()
+    for copy in copies:
+        copy.start()
     lane = lax.broadcasted_iota(jnp.int32, (width, modes), 1)
     sign = jnp.where(lane % 2 == 0, 1.0, -1.0)
-    table = table_ref[...]
-    width_x = field_ref.shape[1]
+    table_copy.wait()
     for pair in range(0, width_x, 2):
+        copies[pair // 2].wait()
         rows = []
         for at in (pair, pair + 1):
-            real, imag = field_ref[0, at], field_ref[1, at]
+            real, imag = field[0, at], field[1, at]
             for factor in (None, sign):
                 if factor is not None:
                     real, imag = real * factor, imag * factor
@@ -44,17 +52,19 @@
                 rows.append(jnp.concatenate([imag, real], axis=1).astype(BF16))
         block = jnp.concatenate(rows, axis=0)
         product = lax.dot_general(
-            table, block, (((1,), (1,)), ((), ())), preferred_element_type=F32
+            table[...], block, (((1,), (1,)), ((), ())), preferred_element_type=F32
         ) * scale
         for k in range(2):
             wide_ref[pl.ds(pair + k, modes, stride=width_x), :] = product[:, 128 * k : 128 * (k + 1)]
     out_ref[...] = wide_ref[...].astype(BF16).reshape(out_ref.shape)
 
 
-def planes(in_ref, ty_ref, tx_ref, fx_ref, fy_ref, out_ref, back_ref, done_ref, *, scale_in, scale_out, chunk):
+def planes(in_ref, ty_ref, tx_ref, fy_ref, out_ref, back_ref, done_ref, *, scale_in, scale_out, chunk):
     modes = 256
     grid = 512
     half = 64
+    fx = tx_ref[...]
+    tx = fx.T
     for plane in range(2):
         parts = []
         for x in range(4):
@@ -68,7 +78,7 @@
             rhs = jnp.concatenate(
                 [along_y[:, start : start + chunk], along_y[:, grid + start : grid + start + chunk]], axis=1
             )
-            even_odd = jnp.dot(tx_ref[...], rhs, preferred_element_type=F32) * scale_in
+            even_odd = jnp.dot(tx, rhs, preferred_element_type=F32) * scale_in
             pr, pi = even_odd[:modes, :chunk], even_odd[:modes, chunk:]
             qr, qi = even_odd[modes:, :chunk], even_odd[modes:, chunk:]
             ar = jnp.where(first, pr, pr - qi)
@@ -89,7 +99,7 @@
                 ],
                 axis=0,
             )
-            back_x = (jnp.dot(fx_ref[...], folded, preferred_element_type=F32) * scale_out).astype(BF16)
+            back_x = (jnp.dot(fx, folded, preferred_element_type=F32) * scale_out).astype(BF16)
             back_ref[:, start : start + chunk] = back_x[:, :chunk]
             back_ref[:, grid + start : grid + start + chunk] = back_x[:, chunk:]
         done_ref[plane] = (
@@ -102,32 +112,43 @@
             out_ref[z, :, x] = message.reshape(16, 16, 128)
 
 
-def finish(in_ref, field_ref, table_ref, out_ref, sums_ref, wide_ref, energy_ref, *, scale, bins):
-    _, width_x, width_y, modes = field_ref.shape
-    half_modes = modes // 2
+def place(width_x, width_y, modes):
     row = (lax.axis_index("z_lo") * 4 + lax.axis_index("y")) * 2 + lax.axis_index("core")
     col = lax.axis_index("x") * 2 + lax.axis_index("z_hi")
-    base_x = row * width_x - half_modes
-    base_y = col * width_y - half_modes
+    return row * width_x - modes // 2, col * width_y - modes // 2
+
+
+def waves_yz(base_y, width_y, modes):
     wave_y = base_y + lax.broadcasted_iota(jnp.int32, (width_y, modes), 0)
-    wave_z = lax.broadcasted_iota(jnp.int32, (width_y, modes), 1) - half_modes
+    wave_z = lax.broadcasted_iota(jnp.int32, (width_y, modes), 1) - modes // 2
+    return wave_y, wave_z
+
+
+def finish(in_ref, field_ref, table_ref, out_hbm, sums_ref, wide_ref, out_ref, energy_ref, shell_ref, sems, *, scale, bins):
+    _, width_x, width_y, modes = field_ref.shape
+    base_x, base_y = place(width_x, width_y, modes)
+    wave_y, wave_z = waves_yz(base_y, width_y, modes)
     square_yz = wave_y * wave_y + wave_z * wave_z
-    angle_yz = phase_rate * square_yz.astype(F32)
-    cos_yz, sin_yz = jnp.cos(angle_yz), jnp.sin(angle_yz)
-    wave_x8 = base_x + lax.broadcasted_iota(jnp.int32, (width_x, modes), 0)
-    angle_x = phase_rate * (wave_x8 * wave_x8).astype(F32)
-    cos_x, sin_x = jnp.cos(angle_x), jnp.sin(angle_x)
     near_x = jnp.maximum(base_x, -(base_x + width_x - 1))
     near_y = jnp.maximum(base_y, -(base_y + width_y - 1))
     near = near_x * near_x + near_y * near_y
 
     def shell_of(squared):
-        return jnp.floor(jnp.sqrt(squared.astype(F32)) + 0.5).astype(jnp.int32)
+        return jnp.floor(jnp.sqrt(squared.astype(F32)) + 0.5)
 
     lowest = shell_of(near + wave_z * wave_z)
+    angle_yz = phase_rate * square_yz.astype(F32)
+    cos_yz, sin_yz = jnp.cos(angle_yz), jnp.sin(angle_yz)
+    wave_x = base_x + lax.broadcasted_iota(jnp.int32, (width_x, modes), 0)
+    angle_x = phase_rate * (wave_x * wave_x).astype(F32)
+    cos_x, sin_x = jnp.cos(angle_x), jnp.sin(angle_x)
     sign = jnp.where(wave_z % 2 == 0, 1.0, -1.0)
     wide_ref[...] = in_ref[...].reshape(wide_ref.shape).astype(F32)
     table = table_ref[...]
+    copies = [
+        pltpu.make_async_copy(out_ref.at[:, pl.ds(at, 1)], out_hbm.at[:, pl.ds(at, 1)], sems.at[at])
+        for at in range(width_x)
+    ]
     for at in range(width_x):
         slab = wide_ref[pl.ds(at, modes, stride=width_x), :].astype(BF16)
         got = lax.dot_general(slab, table, (((0,), (0,)), ((), ())), preferred_element_type=F32)
@@ -143,24 +164,32 @@
         new_i = v * cos - u * sin
         out_ref[0, at] = new_r
         out_ref[1, at] = new_i
-        energy_ref[0, at] = new_r * new_r + new_i * new_i
+        copies[at].start()
+        energy_ref[at] = new_r * new_r + new_i * new_i
         wx = base_x + at
-        energy_ref[1, at] = (shell_of(square_yz + wx * wx) - lowest).astype(F32)
+        shell_ref[at] = shell_of(square_yz + wx * wx) - lowest
     rows = []
     for k in range(bins):
         total = jnp.zeros((8, modes), F32)
         for at in range(width_x):
-            hit = jnp.where(energy_ref[1, at] == float(k), energy_ref[0, at], 0.0)
+            hit = jnp.where(shell_ref[at] == float(k), energy_ref[at], 0.0)
             for j in range(0, width_y, 8):
                 total = total + hit[j : j + 8]
         rows.append(jnp.sum(total, axis=0, keepdims=True))
+    rows.extend([jnp.zeros((1, modes), F32)] * (-bins % 8))
     stacked = jnp.concatenate(rows, axis=0)
-    wave_col = lax.broadcasted_iota(jnp.int32, (modes, modes), 0) - half_modes
-    shell_col = shell_of(near + wave_col * wave_col)
+    wave_col = lax.broadcasted_iota(jnp.int32, (modes, modes), 0) - modes // 2
+    shell_col = shell_of(near + wave_col * wave_col).astype(jnp.int32)
     one_hot = (shell_col == lax.broadcasted_iota(jnp.int32, (modes, modes), 1)).astype(F32)
     placed = jnp.dot(stacked, one_hot, preferred_element_type=F32, precision=lax.Precision.HIGHEST)
     shifted = pltpu.roll(placed, 0, 1, stride=1, stride_axis=0)
     sums_ref[...] = jnp.sum(shifted, axis=0, keepdims=True)
+    for copy in copies:
+        copy.wait()
+
+
+def mean_up(copies_ref, weight_ref, out_ref):
+    out_ref[...] = jnp.sum(copies_ref[...].astype(F32), axis=0) * weight_ref[...]
 
 
 def tables(modes):
@@ -177,8 +206,7 @@
     odd = low_sin.copy()
     odd[0] = cos[:, modes]
     tx = np.concatenate([low_cos, odd], axis=0)
-    fx = tx.T
-    return [jnp.asarray(np.ascontiguousarray(t), BF16) for t in (z_table, ty, tx, fx, fy)]
+    return [jnp.asarray(np.ascontiguousarray(t), BF16) for t in (z_table, ty, tx.T, fy)]
 
 
 def shell_counts(modes):
@@ -198,16 +226,21 @@
     devices = lax.axis_size(RING)
     scale_in = 1.0 / math.sqrt(modes)
     scale_out = math.sqrt(modes) / (2 * modes)
-    z_table, ty, tx, fx, fy = tables(modes)
-    import functools
-
+    z_table, ty, fx, fy = tables(modes)
     messages = pl.pallas_call(
         functools.partial(to_slabs, scale=scale_in),
+        in_specs=[pl.BlockSpec(memory_space=pltpu.HBM)] * 2,
         out_shape=jax.ShapeDtypeStruct((devices, width_x, 128), BF16),
-        scratch_shapes=[pltpu.VMEM((devices * width_x, 128), F32)],
+        scratch_shapes=[
+            pltpu.VMEM((devices * width_x, 128), F32),
+            pltpu.VMEM(field.shape, F32),
+            pltpu.VMEM(z_table.shape, BF16),
+            pltpu.SemaphoreType.DMA((width_x // 2,)),
+            pltpu.SemaphoreType.DMA(()),
+        ],
         compiler_params=params(),
         name="to_slabs",
-    )(field, z_table)
+    )(pltpu.with_memory_space_constraint(field, pltpu.HBM), pltpu.with_memory_space_constraint(z_table, pltpu.HBM))
     slabs = lax.all_to_all(messages, RING, 0, 0, tiled=True)
     back = pl.pallas_call(
         functools.partial(planes, scale_in=scale_in, scale_out=scale_out, chunk=256),
@@ -215,23 +248,31 @@
         scratch_shapes=[pltpu.VMEM((modes, 4 * modes), BF16), pltpu.VMEM((2, modes, 2 * modes), BF16)],
         compiler_params=params(),
         name="planes",
-    )(slabs.reshape(2, 16, 4, 16, 128), ty, tx, fx, fy)
+    )(slabs.reshape(2, 16, 4, 16, 128), ty, fx, fy)
     home = lax.all_to_all(back.reshape(devices, width_x, 128), RING, 0, 0, tiled=True)
-    bins = 8 * math.ceil((math.sqrt((width_x - 1) ** 2 + (width_y - 1) ** 2) + 2) / 8)
+    bins = math.ceil(math.sqrt((width_x - 1) ** 2 + (width_y - 1) ** 2)) + 2
     updated, sums = pl.pallas_call(
         functools.partial(finish, scale=scale_out, bins=bins),
         out_shape=[jax.ShapeDtypeStruct(field.shape, F32), jax.ShapeDtypeStruct((1, modes), F32)],
+        out_specs=[pl.BlockSpec(memory_space=pltpu.HBM), pl.BlockSpec(memory_space=pltpu.VMEM)],
         scratch_shapes=[
             pltpu.VMEM((devices * width_x, 128), F32),
-            pltpu.VMEM((2, width_x, width_y, modes), F32),
+            pltpu.VMEM(field.shape, F32),
+            pltpu.VMEM((width_x, width_y, modes), F32),
+            pltpu.VMEM((width_x, width_y, modes), F32),
+            pltpu.SemaphoreType.DMA((width_x,)),
         ],
         compiler_params=params(),
         name="finish",
     )(home, field, z_table)
-    copies = jnp.broadcast_to(sums.reshape(1, modes // 128, 128), (devices, modes // 128, 128))
+    lanes = modes // 128
+    copies = jnp.broadcast_to(sums.reshape(1, lanes, 128).astype(BF16), (devices, lanes, 128))
     everyone = lax.all_to_all(copies, RING, 0, 0, tiled=True)
-    spectrum = jnp.sum(everyone, axis=0).reshape(modes) / jnp.asarray(np.maximum(shell_counts(modes), 1.0))
-    return updated, spectrum
+    weights = jnp.asarray((1.0 / np.maximum(shell_counts(modes), 1.0)).reshape(lanes, 128))
+    spectrum = pl.pallas_call(
+        mean_up, out_shape=jax.ShapeDtypeStruct((lanes, 128), F32), compiler_params=params(), name="mean_up"
+    )(everyone, weights)
+    return updated, spectrum.reshape(modes)
 
 
 def solution(mesh):

time: 94.6 us -> 91 us (0.962)
  local copies, waits for them, and re-layouts: 3.42 us -> 0.11 us
  Pallas kernels: 6.85 us -> 9.72 us
  blocking collectives: 82.5 us -> 80.2 us
    unnamed x16 -> x12, local copies, waits for them, and re-layouts: 3.35 us -> 0.04 us
    pallas_call x1 -> x2, Pallas kernels: 0.54 us -> 3.49 us  [the longest x1 2.66 us: body(): pl.pallas_call(functools.partial(to_slabs, scale=scale_in), in_specs=[pl....]
    all_to_all x1, blocking collectives: 21.2 us -> 19 us  [body(): everyone = lax.all_to_all(copies, RING, 0, 0, tiled=True)]
where the time goes in v1:
time: 91 us; the launch traced here: 90.8 us
  blocking collectives  80.2 us (88%)
  Pallas kernels  9.72 us (11%)
    all_to_all x1, blocking collectives, body(): slabs = lax.all_to_all(messages, RING, 0, 0, tiled=True)  35.3 us
    all_to_all x1, blocking collectives, body(): lax.all_to_all(back.reshape(devices, width_x, 128), RING, 0, 0, tiled=True)  25.9 us
    all_to_all x1, blocking collectives, body(): everyone = lax.all_to_all(copies, RING, 0, 0, tiled=True)  19 us
    pallas_call x1, Pallas kernels, body(): pl.pallas_call(functools.partial(planes, scale_in=scale_in, scale_out=sca...  3.92 us
    pallas_call x1, Pallas kernels, body(): pl.pallas_call(functools.partial(to_slabs, scale=scale_in), in_specs=[pl....  2.66 us
    pallas_call x1, Pallas kernels, body(): pl.pallas_call(functools.partial(finish, scale=scale_out, bins=bins), out...  2.31 us

profile of v1, /device:TPU:1, one launch (start us, length us, event | category | flops | bytes accessed | tf_op | source)
XLA Modules:
  0.0 90.8 jit_solution(7865842377931264180)
XLA Ops:
  0.6 0.0 copy-start.2
  0.6 0.0 copy-start.3
  0.7 2.7 %to_slabs.1 = bf16[256,8,128]{2,1,0:T(8,128)(2,1)S(1)} custom-call(f32[2,8,32,256]{3,2,1,0:T(8,128)} %field_ref.3, bf16[256,512]{1,0:T(8,128)(2,1)} %constant.10.clone.table_hbm.table_ref), custom_call_target="tpu_custom_call" | custom-call | tf_op jit(solution)/shard_map/to_slabs/pallas_call | solution.py:230
  3.3 0.0 copy-start.4
  3.3 35.3 %all_to_all.15 = bf16[256,8,128]{2,1,0:T(8,128)(2,1)S(1)} all-to-all(bf16[256,8,128]{2,1,0:T(8,128)(2,1)S(1)} %to_slabs.1), channel_id=1, replica_groups=mesh['z_lo'=4,'y'=4,'core'=2,'x'=4,'z_hi'=2] {'z_hi','z_lo','y','x','core'}, dimensions={0} | all-to-all | bytes 1048576 | tf_op jit(solution)/shard_map/all_to_all | solution.py:244
  38.7 0.0 copy-done.2
  38.7 0.0 copy-done.3
  38.7 0.0 copy-done.4
  38.7 3.9 %planes.1 = bf16[2,16,4,16,128]{4,3,2,1,0:T(8,128)(2,1)S(1)} custom-call(bf16[2,16,4,16,128]{4,3,2,1,0:T(8,128)(2,1)S(1)} %bitcast.4, bf16[512,1024]{1,0:T(8,128)(2,1)S(1)} %copy-done.3, bf16[256,512]{1,0:T(8,128)(2,1)S(1)} %copy-done.4, bf16[1024,512]{1,0:T(8,128)(2,1)S(1)} %copy-done.2), custom_call_target="tpu_custom_call" | custom-call | tf_op jit(solution)/shard_map/planes/pallas_call | solution.py:245
  42.6 0.0 copy-start
  42.6 0.0 copy-start.1
  42.6 25.9 %all_to_all.16.in_ref = bf16[256,8,128]{2,1,0:T(8,128)(2,1)S(1)} all-to-all(bf16[256,8,128]{2,1,0:T(8,128)(2,1)S(1)} %bitcast.5), channel_id=1, replica_groups=mesh['z_lo'=4,'y'=4,'core'=2,'x'=4,'z_hi'=2] {'z_hi','z_lo','y','x','core'}, dimensions={0} | all-to-all | bytes 1048576 | tf_op jit(solution)/shard_map/all_to_all | solution.py:252
  68.5 0.0 copy-done
  68.5 0.0 copy-done.1
  68.5 2.3 %finish.1 = (f32[2,8,32,256]{3,2,1,0:T(8,128)}, f32[1,256]{1,0:T(1,128)S(1)}) custom-call(bf16[256,8,128]{2,1,0:T(8,128)(2,1)S(1)} %all_to_all.16.in_ref, f32[2,8,32,256]{3,2,1,0:T(8,128)S(1)} %copy-done, bf16[256,512]{1,0:T(8,128)(2,1)S(1)} %copy-done.1), custom_call_target="tpu_custom_call" | custom-call | tf_op jit(solution)/shard_map/finish/pallas_call | solution.py:254
  70.8 0.1 broadcast_in_dim.2
  70.9 0.0 copy-start.5
  70.9 19.0 %all_to_all.17.copies_ref = bf16[256,2,128]{2,1,0:T(2,128)(2,1)S(1)} all-to-all(bf16[256,2,128]{2,1,0:T(2,128)(2,1)S(1)} %broadcast_in_dim.2), channel_id=1, replica_groups=mesh['z_lo'=4,'y'=4,'core'=2,'x'=4,'z_hi'=2] {'z_hi','z_lo','y','x','core'}, dimensions={0} | all-to-all | bytes 262144 | tf_op jit(solution)/shard_map/all_to_all | solution.py:270
  89.9 0.0 copy-done.5
  89.9 0.8 mean_up.1
  (1 shorter events, 0.0 us)
Async XLA Ops:
  0.6 38.0 %copy-start.2 = (bf16[1024,512]{1,0:T(8,128)(2,1)S(1)}, bf16[1024,512]{1,0:T(8,128)(2,1)}, u32[]{:S(2)}) copy-start(bf16[1024,512]{1,0:T(8,128)(2,1)} %constant.13.clone.fy_ref) | copy-start | bytes 3145732
  0.6 38.0 %copy-start.3 = (bf16[512,1024]{1,0:T(8,128)(2,1)S(1)}, bf16[512,1024]{1,0:T(8,128)(2,1)}, u32[]{:S(2)}) copy-start(bf16[512,1024]{1,0:T(8,128)(2,1)} %constant.11.clone.ty_ref) | copy-start | bytes 3145732
  3.3 35.4 %copy-start.4 = (bf16[256,512]{1,0:T(8,128)(2,1)S(1)}, bf16[256,512]{1,0:T(8,128)(2,1)}, u32[]{:S(2)}) copy-start(bf16[256,512]{1,0:T(8,128)(2,1)} %constant.12.clone.tx_ref) | copy-start | bytes 786436
  42.6 25.9 %copy-start = (f32[2,8,32,256]{3,2,1,0:T(8,128)S(1)}, f32[2,8,32,256]{3,2,1,0:T(8,128)}, u32[]{:S(2)}) copy-start(f32[2,8,32,256]{3,2,1,0:T(8,128)} %field_ref.3) | copy-start | bytes 1572868
  42.6 25.9 %copy-start.1 = (bf16[256,512]{1,0:T(8,128)(2,1)S(1)}, bf16[256,512]{1,0:T(8,128)(2,1)}, u32[]{:S(2)}) copy-start(bf16[256,512]{1,0:T(8,128)(2,1)} %constant.10.clone.table_hbm.table_ref) | copy-start | bytes 786436
  70.9 19.0 %copy-start.5 = (f32[2,128]{1,0:T(2,128)S(1)}, f32[2,128]{1,0:T(2,128)}, u32[]{:S(2)}) copy-start(f32[2,128]{1,0:T(2,128)} %constant.14.clone.weight_ref) | copy-start | bytes 3076

commit v2 on v1

v2 whole, which is shorter than its diff:
```python
import functools
import math

import jax
import jax.numpy as jnp
import numpy as np
from jax import lax
from jax.experimental import pallas as pl
from jax.experimental.pallas import tpu as pltpu
from jax.sharding import Mesh
from jax.sharding import PartitionSpec as P

ROW = ("z_lo1", "z_lo0", "y1", "y0", "core")
COL = ("x1", "x0", "z_hi")
RING = ("z_lo1", "y1", "x1", "z_hi", "z_lo0", "y0", "x0", "core")

phase_rate = 0.0002
coupling = 0.2

F32 = jnp.float32
BF16 = jnp.bfloat16


def trig(waves, points, length):
    turns = np.mod(np.asarray(waves)[:, None] * np.asarray(points)[None, :], length)
    angle = turns.astype(np.float32) * np.float32(2.0 * math.pi / length)
    return np.cos(angle).astype(np.float32), np.sin(angle).astype(np.float32)


def place(width_x, width_y, modes):
    row = functools.reduce(lambda at, axis: 2 * at + lax.axis_index(axis), ROW, 0)
    col = functools.reduce(lambda at, axis: 2 * at + lax.axis_index(axis), COL, 0)
    return row * width_x - modes // 2, col * width_y - modes // 2


def nearest(base, width):
    return jnp.maximum(base, -(base + width - 1))


def shell_of(squared):
    return jnp.floor(jnp.sqrt(squared.astype(F32)) + 0.5)


def phases(angle):
    return jnp.cos(angle), jnp.sin(angle)


def geometry(turn_ref, shell_ref, spot_ref):
    _, width_x, width_y, modes = turn_ref.shape
    base_x, base_y = place(width_x, width_y, modes)

    def square(shape, axis, base):
        wave = base + lax.broadcasted_iota(jnp.int32, shape, axis)
        return wave * wave

    square_x = square((width_x, modes), 0, base_x)
    square_y = square((width_y, modes), 0, base_y)
    square_z = square((8, modes), 1, -(modes // 2))
    cos_x, sin_x = phases(phase_rate * square_x[:, :128].astype(F32))
    cos_y, sin_y = phases(phase_rate * square_y[:, :128].astype(F32))
    cos_z, sin_z = phases(phase_rate * square_z.astype(F32))
    cos_x, sin_x, cos_y, sin_y = (jnp.concatenate([t] * (modes // 128), axis=1) for t in (cos_x, sin_x, cos_y, sin_y))
    column = square((modes, modes), 0, -(modes // 2))
    shells = lax.broadcasted_iota(jnp.int32, (modes, modes), 1).astype(F32)
    near_x = nearest(base_x, width_x)
    for block in range(width_y // 8):
        rows = slice(8 * block, 8 * block + 8)
        near_y = nearest(base_y + 8 * block, 8)
        near = near_x * near_x + near_y * near_y
        lowest = shell_of(near + square_z)
        spot_ref[block] = jnp.where(shell_of(near + column) == shells, 1.0, 0.0).astype(BF16)
        cos_yz = cos_y[rows] * cos_z - sin_y[rows] * sin_z
        sin_yz = sin_y[rows] * cos_z + cos_y[rows] * sin_z
        square_yz = square_y[rows] + square_z
        for at in range(width_x):
            cx, sx = cos_x[at : at + 1], sin_x[at : at + 1]
            turn_ref[0, at, rows] = cos_yz * cx - sin_yz * sx
            turn_ref[1, at, rows] = sin_yz * cx + cos_yz * sx
            shell_ref[at, rows] = shell_of(square_yz + square_x[at : at + 1]) - lowest


def to_slabs(
    field_hbm, table_hbm, out_ref, turn_ref, shell_ref, spot_ref, wide_ref, field, table, field_sems, table_sem, *, scale
):
    _, width_x, width, modes = field_hbm.shape
    table_copy = pltpu.make_async_copy(table_hbm, table, table_sem)
    copies = [
        pltpu.make_async_copy(field_hbm.at[:, pl.ds(at, 2)], field.at[:, pl.ds(at, 2)], field_sems.at[at // 2])
        for at in range(0, width_x, 2)
    ]
    table_copy.start()
    for copy in copies:
        copy.start()
    geometry(turn_ref, shell_ref, spot_ref)
    lane = lax.broadcasted_iota(jnp.int32, (width, modes), 1)
    sign = jnp.where(lane % 2 == 0, 1.0, -1.0)
    table_copy.wait()
    for pair in range(0, width_x, 2):
        copies[pair // 2].wait()
        rows = []
        for at in (pair, pair + 1):
            real, imag = field[0, at], field[1, at]
            for factor in (None, sign):
                if factor is not None:
                    real, imag = real * factor, imag * factor
                rows.append(jnp.concatenate([real, -imag], axis=1).astype(BF16))
                rows.append(jnp.concatenate([imag, real], axis=1).astype(BF16))
        block = jnp.concatenate(rows, axis=0)
        product = lax.dot_general(
            table[...], block, (((1,), (1,)), ((), ())), preferred_element_type=F32
        ) * scale
        for k in range(2):
            wide_ref[pl.ds(pair + k, modes, stride=width_x), :] = product[:, 128 * k : 128 * (k + 1)]
    out_ref[...] = wide_ref[...].astype(BF16).reshape(out_ref.shape)


def dot(left, right):
    return jnp.dot(left, right, preferred_element_type=F32)


def cube(parts, head):
    pr, pi, qr, qi = parts
    if head:
        first = lax.broadcasted_iota(jnp.int32, pr.shape, 0) == 0
        pick = functools.partial(jnp.where, first)
    else:
        pick = lambda special, general: general
    ar, ai = pick(pr, pr - qi), pick(pi, pi + qr)
    br, bi = pick(qr, pr + qi), pick(qi, pi - qr)
    ma = coupling * (ar * ar + ai * ai)
    mb = coupling * (br * br + bi * bi)
    ar, ai, br, bi = ma * ar, ma * ai, mb * br, mb * bi
    folded = pick(ar, ar + br), pick(ai, ai + bi), pick(br, ai - bi), pick(bi, br - ar)
    return [part.astype(BF16) for part in folded]


def planes(in_ref, ty_ref, fx_ref, fy_hbm, out_ref, back_ref, fy_ref, fy_sem, *, chunk):
    modes = fx_ref.shape[0]
    grid = 2 * modes
    half = 64
    fy_copy = pltpu.make_async_copy(fy_hbm, fy_ref, fy_sem)
    fy_copy.start()
    fx = fx_ref[...]
    tx = fx.T
    spots = [(x1, x0, z) for x1 in range(2) for x0 in range(2) for z in range(2)]
    blocks = [in_ref[:, x1, z, :, x0].reshape(modes, 128) for x1, x0, z in spots]
    lines = jnp.concatenate(
        [jnp.concatenate([b[:, half * plane : half * (plane + 1)] for b in blocks], axis=1) for plane in range(2)], axis=0
    )
    along_y = dot(lines, ty_ref[...]).astype(BF16)
    for plane in range(2):
        mine = slice(plane * modes, (plane + 1) * modes)
        for start in range(0, grid, chunk):
            real, imag = slice(start, start + chunk), slice(grid + start, grid + start + chunk)
            even_odd = dot(tx, jnp.concatenate([along_y[mine, real], along_y[mine, imag]], axis=1))
            even, odd = even_odd[:modes], even_odd[modes:]
            parts = even[:, :chunk], even[:, chunk:], odd[:, :chunk], odd[:, chunk:]
            top, rest = cube([p[:16] for p in parts], True), cube([p[16:] for p in parts], False)
            even_r, even_i, odd_i, odd_r = (jnp.concatenate(pair, axis=0) for pair in zip(top, rest))
            folded = jnp.concatenate(
                [jnp.concatenate([even_r, even_i], axis=1), jnp.concatenate([odd_i, odd_r], axis=1)], axis=0
            )
            back_x = dot(fx, folded).astype(BF16)
            back_ref[mine, real] = back_x[:, :chunk]
            back_ref[mine, imag] = back_x[:, chunk:]
    fy_copy.wait()
    done = dot(back_ref[...], fy_ref[...]).astype(BF16)
    for k, (x1, x0, z) in enumerate(spots):
        at = slice(half * k, half * (k + 1))
        message = jnp.concatenate([done[:modes, at], done[modes:, at]], axis=1)
        out_ref[:, x1, z, :, x0] = message.reshape(4, 4, 16, 128)


def finish(
    in_ref, field_ref, table_ref, turn_ref, shell_ref, spot_ref, out_hbm, sums_ref, wide_ref, out_ref, energy_ref, sems, *, scale, bins
):
    _, width_x, width_y, modes = field_ref.shape
    lane = lax.broadcasted_iota(jnp.int32, (width_y, modes), 1)
    sign = jnp.where(lane % 2 == 0, 1.0, -1.0)
    wide_ref[...] = in_ref[...].reshape(wide_ref.shape).astype(F32)
    table = table_ref[...]
    copies = [
        pltpu.make_async_copy(out_ref.at[:, pl.ds(at, 1)], out_hbm.at[:, pl.ds(at, 1)], sems.at[at])
        for at in range(width_x)
    ]
    for at in range(width_x):
        slab = wide_ref[pl.ds(at, modes, stride=width_x), :].astype(BF16)
        got = lax.dot_general(slab, table, (((0,), (0,)), ((), ())), preferred_element_type=F32)
        r0, i0, r1, i1 = (got[width_y * k : width_y * (k + 1)] for k in range(4))
        non_r = (r0[:, :modes] + i0[:, modes:] + sign * (r1[:, :modes] + i1[:, modes:])) * scale
        non_i = (i0[:, :modes] - r0[:, modes:] + sign * (i1[:, :modes] - r1[:, modes:])) * scale
        u = field_ref[0, at] - non_i
        v = field_ref[1, at] + non_r
        cos, sin = turn_ref[0, at], turn_ref[1, at]
        new_r = u * cos + v * sin
        new_i = v * cos - u * sin
        out_ref[0, at] = new_r
        out_ref[1, at] = new_i
        copies[at].start()
        energy_ref[at] = new_r * new_r + new_i * new_i
    result = jnp.zeros((1, modes), F32)
    for block in range(width_y // 8):
        rows = slice(8 * block, 8 * block + 8)
        totals = []
        for k in range(bins):
            total = jnp.zeros((8, modes), F32)
            for at in range(width_x):
                total = total + jnp.where(shell_ref[at, rows] == float(k), energy_ref[at, rows], 0.0)
            totals.append(jnp.sum(total, axis=0, keepdims=True))
        totals.extend([jnp.zeros((1, modes), F32)] * (-bins % 16))
        stacked = jnp.concatenate(totals, axis=0)
        high = stacked.astype(BF16)
        left = stacked - high.astype(F32)
        middle = left.astype(BF16)
        low = (left - middle.astype(F32)).astype(BF16)
        placed = dot(jnp.concatenate([high, middle, low], axis=0), spot_ref[block])
        count = stacked.shape[0]
        placed = placed[:count] + placed[count : 2 * count] + placed[2 * count :]
        shifted = pltpu.roll(placed, 0, 1, stride=1, stride_axis=0)
        result = result + jnp.sum(shifted, axis=0, keepdims=True)
    sums_ref[...] = result
    for copy in copies:
        copy.wait()


def mean_up(copies_ref, weight_ref, out_ref):
    out_ref[...] = jnp.sum(copies_ref[...].astype(F32), axis=0) * weight_ref[...]


def tables(modes, scale_in, scale_out):
    grid = 2 * modes
    waves = np.arange(modes) - modes // 2
    cos, sin = trig(waves, np.arange(grid), grid)
    low_cos, low_sin = cos[:, :modes].T, sin[:, :modes].T
    z_table = np.concatenate([low_cos, low_sin], axis=1)
    blocks = modes // 32
    c, s = cos.reshape(blocks, 32, grid), sin.reshape(blocks, 32, grid)
    ty = np.stack([np.concatenate([c, s], 2), np.concatenate([-s, c], 2)], 1).reshape(2 * modes, 2 * grid)
    ct, st = c.transpose(2, 0, 1), s.transpose(2, 0, 1)
    fy = np.stack([np.stack([ct, -st], 2), np.stack([st, ct], 2)], 0).reshape(2 * grid, 2 * modes)
    odd = low_sin.copy()
    odd[0] = cos[:, modes]
    tx = np.concatenate([low_cos, odd], axis=0)
    bits = np.arange(modes).reshape(2, 2, 2, 2, 2, modes // 32)
    fx = tx.T[bits.transpose(0, 2, 1, 3, 4, 5).reshape(-1)]
    scaled = (z_table, ty * scale_in, fx * scale_in, fy * (scale_out * scale_out / scale_in))
    return [jnp.asarray(np.ascontiguousarray(t), BF16) for t in scaled]


def shell_counts(modes):
    wave = np.arange(modes) - modes // 2
    square = wave * wave
    total = square[:, None, None] + square[None, :, None] + square[None, None, :]
    shell = np.floor(np.sqrt(total.astype(np.float32)) + np.float32(0.5)).astype(np.int64)
    return np.bincount(shell.reshape(-1), minlength=modes)[:modes].astype(np.float32)


def in_hbm(array):
    return pltpu.with_memory_space_constraint(array, pltpu.HBM)


def params():
    return pltpu.CompilerParams(vmem_limit_bytes=48 * 1024 * 1024)


def body(field):
    _, width_x, width_y, modes = field.shape
    devices = math.prod(lax.axis_size(axis) for axis in RING)
    scale_in = 1.0 / math.sqrt(modes)
    scale_out = math.sqrt(modes) / (2 * modes)
    z_table, ty, fx, fy = tables(modes, scale_in, scale_out)
    messages, turn, shell, spot = pl.pallas_call(
        functools.partial(to_slabs, scale=scale_in),
        in_specs=[pl.BlockSpec(memory_space=pltpu.HBM)] * 2,
        out_shape=[
            jax.ShapeDtypeStruct((devices, width_x, 128), BF16),
            jax.ShapeDtypeStruct(field.shape, F32),
            jax.ShapeDtypeStruct(field.shape[1:], F32),
            jax.ShapeDtypeStruct((width_y // 8, modes, modes), BF16),
        ],
        scratch_shapes=[
            pltpu.VMEM((devices * width_x, 128), F32),
            pltpu.VMEM(field.shape, F32),
            pltpu.VMEM(z_table.shape, BF16),
            pltpu.SemaphoreType.DMA((width_x // 2,)),
            pltpu.SemaphoreType.DMA(()),
        ],
        compiler_params=params(),
        name="to_slabs",
    )(in_hbm(field), in_hbm(z_table))
    slabs = lax.all_to_all(messages, RING, 0, 0, tiled=True)
    shape = (4, 2, 2, 4, 2, 2 * width_x, 128)
    back = pl.pallas_call(
        functools.partial(planes, chunk=128),
        in_specs=[pl.BlockSpec(memory_space=pltpu.VMEM)] * 3 + [pl.BlockSpec(memory_space=pltpu.HBM)],
        out_shape=jax.ShapeDtypeStruct(shape, BF16),
        scratch_shapes=[
            pltpu.VMEM((2 * modes, 4 * modes), BF16),
            pltpu.VMEM(fy.shape, BF16),
            pltpu.SemaphoreType.DMA(()),
        ],
        compiler_params=params(),
        name="planes",
    )(slabs.reshape(shape), ty, fx, in_hbm(fy))
    home = lax.all_to_all(back.reshape(devices, width_x, 128), RING, 0, 0, tiled=True)
    bins = math.ceil(math.sqrt((width_x - 1) ** 2 + 49)) + 2
    updated, sums = pl.pallas_call(
        functools.partial(finish, scale=scale_out, bins=bins),
        out_shape=[jax.ShapeDtypeStruct(field.shape, F32), jax.ShapeDtypeStruct((1, modes), F32)],
        out_specs=[pl.BlockSpec(memory_space=pltpu.HBM), pl.BlockSpec(memory_space=pltpu.VMEM)],
        scratch_shapes=[
            pltpu.VMEM((devices * width_x, 128), F32),
            pltpu.VMEM(field.shape, F32),
            pltpu.VMEM((width_x, width_y, modes), F32),
            pltpu.SemaphoreType.DMA((width_x,)),
        ],
        compiler_params=params(),
        name="finish",
    )(home, field, z_table, turn, shell, spot)
    lanes = modes // 128
    copies = jnp.broadcast_to(sums.reshape(1, lanes, 128).astype(BF16), (devices, lanes, 128))
    everyone = lax.all_to_all(copies, RING, 0, 0, tiled=True)
    weights = jnp.asarray((1.0 / np.maximum(shell_counts(modes), 1.0)).reshape(lanes, 128))
    spectrum = pl.pallas_call(
        mean_up, out_shape=jax.ShapeDtypeStruct((lanes, 128), F32), compiler_params=params(), name="mean_up"
    )(everyone, weights)
    return updated, spectrum.reshape(modes)


def solution(mesh):
    split = Mesh(mesh.devices.reshape((2,) * 8), ROW + COL)
    placed = (P(None, ROW, COL, None),)
    return jax.shard_map(
        body, mesh=split, in_specs=placed, out_specs=(P(None, ROW, COL, None), P()), check_vma=False
    )
```

time: 91 us -> 90.5 us (level)
    pallas_call x1, Pallas kernels: 2.31 us -> 1.32 us  [body(): pl.pallas_call(functools.partial(finish, scale=scale_out, bins=bins), out...]
where the time goes in v2:
time: 90.5 us; the launch traced here: 90.3 us
  blocking collectives  80.6 us (89%)
  Pallas kernels  8.87 us (10%)
    all_to_all x1, blocking collectives, body(): slabs = lax.all_to_all(messages, RING, 0, 0, tiled=True)  35.5 us
    all_to_all x1, blocking collectives, body(): lax.all_to_all(back.reshape(devices, width_x, 128), RING, 0, 0, tiled=True)  26.2 us
    all_to_all x1, blocking collectives, body(): everyone = lax.all_to_all(copies, RING, 0, 0, tiled=True)  18.9 us
    pallas_call x1, Pallas kernels, body(): pl.pallas_call(functools.partial(planes, chunk=128), in_specs=[pl.BlockSp...  4.12 us
    pallas_call x1, Pallas kernels, body(): pl.pallas_call(functools.partial(to_slabs, scale=scale_in), in_specs=[pl....  2.6 us

profile of v2, /device:TPU:1, one launch (start us, length us, event | category | flops | bytes accessed | tf_op | source)
XLA Modules:
  0.0 90.3 jit_solution(3388242681302242865)
XLA Ops:
  0.6 0.0 copy-start.2
  0.6 2.6 %to_slabs.1 = (bf16[256,8,128]{2,1,0:T(8,128)(2,1)S(1)}, f32[2,8,32,256]{3,2,1,0:T(8,128)S(1)}, f32[8,32,256]{2,1,0:T(8,128)S(1)}, bf16[4,256,256]{2,1,0:T(8,128)(2,1)S(1)}) custom-call(f32[2,8,32,256]{3,2,1,0:T(8,128)} %field_ref.1, bf16[256,512]{1,0:T(8,128)(2,1)} %constant.10.clone.table_hbm.table_ref), custom_call_target="tpu_custom_call" | custom-call | tf_op jit(solution)/shard_map/to_slabs/pallas_call | solution.py:272
  3.2 0.0 copy-start.3
  3.3 35.5 %all_to_all.15 = bf16[256,8,128]{2,1,0:T(8,128)(2,1)S(1)} all-to-all(bf16[256,8,128]{2,1,0:T(8,128)(2,1)S(1)} %get-tuple-element.8), channel_id=1, replica_groups=mesh['z_lo1'=2,'z_lo0'=2,'y1'=2,'y0'=2,'core'=2,'x1'=2,'x0'=2,'z_hi'=2] ..., dimensions={0} | all-to-all | bytes 1048576 | tf_op jit(solution)/shard_map/all_to_all | solution.py:291
  38.7 0.0 copy-done.2
  38.7 0.0 copy-done.3
  38.7 4.1 %planes.1 = bf16[4,2,2,4,2,16,128]{6,5,4,3,2,1,0:T(8,128)(2,1)S(1)} custom-call(bf16[4,2,2,4,2,16,128]{6,5,4,3,2,1,0:T(8,128)(2,1)S(1)} %bitcast.4, bf16[512,1024]{1,0:T(8,128)(2,1)S(1)} %copy-done.2, bf16[256,512]{1,0:T(8,128)(2,1)S(1)} %copy-done.3, bf16[1024,512]{1,0:T(8,128)(2,1)} %constant.13.clone.fy_hbm), custom_call_target="tpu_custom_call" | custom-call | tf_op jit(solution)/shard_map/planes/pallas_call | solution.py:293
  42.9 0.0 copy-start
  42.9 0.0 copy-start.1
  42.9 26.2 %all_to_all.16.in_ref = bf16[256,8,128]{2,1,0:T(8,128)(2,1)S(1)} all-to-all(bf16[256,8,128]{2,1,0:T(8,128)(2,1)S(1)} %bitcast.5), channel_id=1, replica_groups=mesh['z_lo1'=2,'z_lo0'=2,'y1'=2,'y0'=2,'core'=2,'x1'=2,'x0'=2,'z_hi'=2] ..., dimensions={0} | all-to-all | bytes 1048576 | tf_op jit(solution)/shard_map/all_to_all | solution.py:305
  69.1 0.0 copy-done
  69.1 0.0 copy-done.1
  69.1 1.3 %finish.1 = (f32[2,8,32,256]{3,2,1,0:T(8,128)}, f32[1,256]{1,0:T(1,128)S(1)}) custom-call(bf16[256,8,128]{2,1,0:T(8,128)(2,1)S(1)} %all_to_all.16.in_ref, f32[2,8,32,256]{3,2,1,0:T(8,128)S(1)} %copy-done, bf16[256,512]{1,0:T(8,128)(2,1)S(1)} %copy-done.1, f32[2,8,32,256]{3,2,1,0:T(8,128)S(1)} %get-tuple-element.9.turn_ref, ...), custom_call_target="tpu_custom_call" | custom-call | tf_op jit(solution)/shard_map/finish/pallas_call | solution.py:307
  70.4 0.1 broadcast_in_dim.2
  70.5 0.0 copy-start.4
  70.5 18.9 %all_to_all.17.copies_ref = bf16[256,2,128]{2,1,0:T(2,128)(2,1)S(1)} all-to-all(bf16[256,2,128]{2,1,0:T(2,128)(2,1)S(1)} %broadcast_in_dim.2), channel_id=1, replica_groups=mesh['z_lo1'=2,'z_lo0'=2,'y1'=2,'y0'=2,'core'=2,'x1'=2,'x0'=2,'z_hi'=2] ..., dimensions={0} | all-to-all | bytes 262144 | tf_op jit(solution)/shard_map/all_to_all | solution.py:322
  89.4 0.0 copy-done.4
  89.4 0.8 mean_up.1
  (1 shorter events, 0.0 us)
Async XLA Ops:
  0.6 38.1 %copy-start.2 = (bf16[512,1024]{1,0:T(8,128)(2,1)S(1)}, bf16[512,1024]{1,0:T(8,128)(2,1)}, u32[]{:S(2)}) copy-start(bf16[512,1024]{1,0:T(8,128)(2,1)} %constant.11.clone.ty_ref) | copy-start | bytes 3145732
  3.2 35.5 %copy-start.3 = (bf16[256,512]{1,0:T(8,128)(2,1)S(1)}, bf16[256,512]{1,0:T(8,128)(2,1)}, u32[]{:S(2)}) copy-start(bf16[256,512]{1,0:T(8,128)(2,1)} %constant.12.clone.fx_ref) | copy-start | bytes 786436
  42.9 26.2 %copy-start = (f32[2,8,32,256]{3,2,1,0:T(8,128)S(1)}, f32[2,8,32,256]{3,2,1,0:T(8,128)}, u32[]{:S(2)}) copy-start(f32[2,8,32,256]{3,2,1,0:T(8,128)} %field_ref.1) | copy-start | bytes 1572868
  42.9 26.2 %copy-start.1 = (bf16[256,512]{1,0:T(8,128)(2,1)S(1)}, bf16[256,512]{1,0:T(8,128)(2,1)}, u32[]{:S(2)}) copy-start(bf16[256,512]{1,0:T(8,128)(2,1)} %constant.10.clone.table_hbm.table_ref) | copy-start | bytes 786436
  70.5 18.9 %copy-start.4 = (f32[2,128]{1,0:T(2,128)S(1)}, f32[2,128]{1,0:T(2,128)}, u32[]{:S(2)}) copy-start(f32[2,128]{1,0:T(2,128)} %constant.14.clone.weight_ref) | copy-start | bytes 3076

commit v3 on v2

--- a/solution.py
+++ b/solution.py
@@ -80,23 +80,19 @@
 
 
 def to_slabs(
-    field_hbm, table_hbm, out_ref, turn_ref, shell_ref, spot_ref, wide_ref, field, table, field_sems, table_sem, *, scale
+    field_hbm, table_hbm, ty_hbm, fy_hbm, out_ref, turn_ref, shell_ref, spot_ref, ty_ref, fy_ref, wide_ref, field, table, sems, *, scale
 ):
     _, width_x, width, modes = field_hbm.shape
-    table_copy = pltpu.make_async_copy(table_hbm, table, table_sem)
-    copies = [
-        pltpu.make_async_copy(field_hbm.at[:, pl.ds(at, 2)], field.at[:, pl.ds(at, 2)], field_sems.at[at // 2])
-        for at in range(0, width_x, 2)
-    ]
-    table_copy.start()
+    pairs = (table_hbm, table), (field_hbm, field), (ty_hbm, ty_ref), (fy_hbm, fy_ref)
+    copies = [pltpu.make_async_copy(source, target, sems.at[k]) for k, (source, target) in enumerate(pairs)]
     for copy in copies:
         copy.start()
     geometry(turn_ref, shell_ref, spot_ref)
     lane = lax.broadcasted_iota(jnp.int32, (width, modes), 1)
     sign = jnp.where(lane % 2 == 0, 1.0, -1.0)
-    table_copy.wait()
+    copies[0].wait()
+    copies[1].wait()
     for pair in range(0, width_x, 2):
-        copies[pair // 2].wait()
         rows = []
         for at in (pair, pair + 1):
             real, imag = field[0, at], field[1, at]
@@ -112,6 +108,8 @@
         for k in range(2):
             wide_ref[pl.ds(pair + k, modes, stride=width_x), :] = product[:, 128 * k : 128 * (k + 1)]
     out_ref[...] = wide_ref[...].astype(BF16).reshape(out_ref.shape)
+    copies[2].wait()
+    copies[3].wait()
 
 
 def dot(left, right):
@@ -134,12 +132,10 @@
     return [part.astype(BF16) for part in folded]
 
 
-def planes(in_ref, ty_ref, fx_ref, fy_hbm, out_ref, back_ref, fy_ref, fy_sem, *, chunk):
+def planes(in_ref, ty_ref, fx_ref, fy_ref, out_ref, back_ref, *, chunk):
     modes = fx_ref.shape[0]
     grid = 2 * modes
     half = 64
-    fy_copy = pltpu.make_async_copy(fy_hbm, fy_ref, fy_sem)
-    fy_copy.start()
     fx = fx_ref[...]
     tx = fx.T
     spots = [(x1, x0, z) for x1 in range(2) for x0 in range(2) for z in range(2)]
@@ -163,7 +159,6 @@
             back_x = dot(fx, folded).astype(BF16)
             back_ref[mine, real] = back_x[:, :chunk]
             back_ref[mine, imag] = back_x[:, chunk:]
-    fy_copy.wait()
     done = dot(back_ref[...], fy_ref[...]).astype(BF16)
     for k, (x1, x0, z) in enumerate(spots):
         at = slice(half * k, half * (k + 1))
@@ -269,39 +264,35 @@
     scale_in = 1.0 / math.sqrt(modes)
     scale_out = math.sqrt(modes) / (2 * modes)
     z_table, ty, fx, fy = tables(modes, scale_in, scale_out)
-    messages, turn, shell, spot = pl.pallas_call(
+    messages, turn, shell, spot, near_ty, near_fy = pl.pallas_call(
         functools.partial(to_slabs, scale=scale_in),
-        in_specs=[pl.BlockSpec(memory_space=pltpu.HBM)] * 2,
+        in_specs=[pl.BlockSpec(memory_space=pltpu.HBM)] * 4,
         out_shape=[
             jax.ShapeDtypeStruct((devices, width_x, 128), BF16),
             jax.ShapeDtypeStruct(field.shape, F32),
             jax.ShapeDtypeStruct(field.shape[1:], F32),
             jax.ShapeDtypeStruct((width_y // 8, modes, modes), BF16),
+            jax.ShapeDtypeStruct(ty.shape, BF16),
+            jax.ShapeDtypeStruct(fy.shape, BF16),
         ],
         scratch_shapes=[
             pltpu.VMEM((devices * width_x, 128), F32),
             pltpu.VMEM(field.shape, F32),
             pltpu.VMEM(z_table.shape, BF16),
-            pltpu.SemaphoreType.DMA((width_x // 2,)),
-            pltpu.SemaphoreType.DMA(()),
+            pltpu.SemaphoreType.DMA((4,)),
         ],
         compiler_params=params(),
         name="to_slabs",
-    )(in_hbm(field), in_hbm(z_table))
+    )(in_hbm(field), in_hbm(z_table), in_hbm(ty), in_hbm(fy))
     slabs = lax.all_to_all(messages, RING, 0, 0, tiled=True)
     shape = (4, 2, 2, 4, 2, 2 * width_x, 128)
     back = pl.pallas_call(
         functools.partial(planes, chunk=128),
-        in_specs=[pl.BlockSpec(memory_space=pltpu.VMEM)] * 3 + [pl.BlockSpec(memory_space=pltpu.HBM)],
         out_shape=jax.ShapeDtypeStruct(shape, BF16),
-        scratch_shapes=[
-            pltpu.VMEM((2 * modes, 4 * modes), BF16),
-            pltpu.VMEM(fy.shape, BF16),
-            pltpu.SemaphoreType.DMA(()),
-        ],
+        scratch_shapes=[pltpu.VMEM((2 * modes, 4 * modes), BF16)],
         compiler_params=params(),
         name="planes",
-    )(slabs.reshape(shape), ty, fx, in_hbm(fy))
+    )(slabs.reshape(shape), near_ty, fx, near_fy)
     home = lax.all_to_all(back.reshape(devices, width_x, 128), RING, 0, 0, tiled=True)
     bins = math.ceil(math.sqrt((width_x - 1) ** 2 + 49)) + 2
     updated, sums = pl.pallas_call(

time: 90.5 us -> 88.5 us (0.978)
  Pallas kernels: 8.87 us -> 6.9 us
    pallas_call x1, Pallas kernels: 4.12 us -> 2.92 us  [body(): pl.pallas_call(functools.partial(planes, chunk=128), out_shape=jax.ShapeD...]
where the time goes in v3:
time: 88.5 us; the launch traced here: 88.3 us
  blocking collectives  80.6 us (91%)
  Pallas kernels  6.9 us (8%)
    all_to_all x1, blocking collectives, body(): slabs = lax.all_to_all(messages, RING, 0, 0, tiled=True)  35.5 us
    all_to_all x1, blocking collectives, body(): lax.all_to_all(back.reshape(devices, width_x, 128), RING, 0, 0, tiled=True)  26.2 us
    all_to_all x1, blocking collectives, body(): everyone = lax.all_to_all(copies, RING, 0, 0, tiled=True)  18.9 us
    pallas_call x1, Pallas kernels, body(): pl.pallas_call(functools.partial(planes, chunk=128), out_shape=jax.ShapeD...  2.92 us
    pallas_call x1, Pallas kernels, body(): pl.pallas_call(functools.partial(to_slabs, scale=scale_in), in_specs=[pl....  1.83 us

profile of v3, /device:TPU:1, one launch (start us, length us, event | category | flops | bytes accessed | tf_op | source)
XLA Modules:
  0.0 88.3 jit_solution(16382545634759024709)
XLA Ops:
  0.6 1.8 %to_slabs.1 = (bf16[256,8,128]{2,1,0:T(8,128)(2,1)S(1)}, f32[2,8,32,256]{3,2,1,0:T(8,128)S(1)}, f32[8,32,256]{2,1,0:T(8,128)S(1)}, bf16[4,256,256]{2,1,0:T(8,128...) custom-call(f32[2,8,32,256]{3,2,1,0:T(8,128)} %field_ref.1, ...), custom_call_target="tpu_custom_call" | custom-call | tf_op jit(solution)/shard_map/to_slabs/pallas_call | solution.py:267
  2.5 0.0 copy-start.2
  2.5 35.5 %all_to_all.15 = bf16[256,8,128]{2,1,0:T(8,128)(2,1)S(1)} all-to-all(bf16[256,8,128]{2,1,0:T(8,128)(2,1)S(1)} %get-tuple-element.10), channel_id=1, replica_groups=mesh['z_lo1'=2,'z_lo0'=2,'y1'=2,'y0'=2,'core'=2,'x1'=2,'x0'=2,'z_hi'=2] ..., dimensions={0} | all-to-all | bytes 1048576 | tf_op jit(solution)/shard_map/all_to_all | solution.py:287
  37.9 0.0 copy-done.2
  37.9 2.9 %planes.1 = bf16[4,2,2,4,2,16,128]{6,5,4,3,2,1,0:T(8,128)(2,1)S(1)} custom-call(bf16[4,2,2,4,2,16,128]{6,5,4,3,2,1,0:T(8,128)(2,1)S(1)} %bitcast.4, bf16[512,1024]{1,0:T(8,128)(2,1)S(1)} %get-tuple-element.11.ty_ref, bf16[256,512]{1,0:T(8,128)(2,1)S(1)} %copy-done.2, bf16[1024,512]{1,0:T(8,128)(2,1)S(1)} %get-tuple-element.12.fy_ref), custom_call_target="tpu_custom_call" | custom-call | tf_op jit(solution)/shard_map/planes/pallas_call | solution.py:289
  40.9 0.0 copy-start
  40.9 0.0 copy-start.1
  40.9 26.2 %all_to_all.16.in_ref = bf16[256,8,128]{2,1,0:T(8,128)(2,1)S(1)} all-to-all(bf16[256,8,128]{2,1,0:T(8,128)(2,1)S(1)} %bitcast.5), channel_id=1, replica_groups=mesh['z_lo1'=2,'z_lo0'=2,'y1'=2,'y0'=2,'core'=2,'x1'=2,'x0'=2,'z_hi'=2] ..., dimensions={0} | all-to-all | bytes 1048576 | tf_op jit(solution)/shard_map/all_to_all | solution.py:296
  67.1 0.0 copy-done
  67.1 0.0 copy-done.1
  67.1 1.3 %finish.1 = (f32[2,8,32,256]{3,2,1,0:T(8,128)}, f32[1,256]{1,0:T(1,128)S(1)}) custom-call(bf16[256,8,128]{2,1,0:T(8,128)(2,1)S(1)} %all_to_all.16.in_ref, f32[2,8,32,256]{3,2,1,0:T(8,128)S(1)} %copy-done, bf16[256,512]{1,0:T(8,128)(2,1)S(1)} %copy-done.1, f32[2,8,32,256]{3,2,1,0:T(8,128)S(1)} %get-tuple-element.13.turn_ref, ...), custom_call_target="tpu_custom_call" | custom-call | tf_op jit(solution)/shard_map/finish/pallas_call | solution.py:298
  68.4 0.1 broadcast_in_dim.2
  68.5 0.0 copy-start.3
  68.5 18.9 %all_to_all.17.copies_ref = bf16[256,2,128]{2,1,0:T(2,128)(2,1)S(1)} all-to-all(bf16[256,2,128]{2,1,0:T(2,128)(2,1)S(1)} %broadcast_in_dim.2), channel_id=1, replica_groups=mesh['z_lo1'=2,'z_lo0'=2,'y1'=2,'y0'=2,'core'=2,'x1'=2,'x0'=2,'z_hi'=2] ..., dimensions={0} | all-to-all | bytes 262144 | tf_op jit(solution)/shard_map/all_to_all | solution.py:313
  87.4 0.0 copy-done.3
  87.5 0.8 mean_up.1
  (1 shorter events, 0.0 us)
Async XLA Ops:
  2.5 35.5 %copy-start.2 = (bf16[256,512]{1,0:T(8,128)(2,1)S(1)}, bf16[256,512]{1,0:T(8,128)(2,1)}, u32[]{:S(2)}) copy-start(bf16[256,512]{1,0:T(8,128)(2,1)} %constant.12.clone.fx_ref) | copy-start | bytes 786436
  40.9 26.2 %copy-start = (f32[2,8,32,256]{3,2,1,0:T(8,128)S(1)}, f32[2,8,32,256]{3,2,1,0:T(8,128)}, u32[]{:S(2)}) copy-start(f32[2,8,32,256]{3,2,1,0:T(8,128)} %field_ref.1) | copy-start | bytes 1572868
  40.9 26.2 %copy-start.1 = (bf16[256,512]{1,0:T(8,128)(2,1)S(1)}, bf16[256,512]{1,0:T(8,128)(2,1)}, u32[]{:S(2)}) copy-start(bf16[256,512]{1,0:T(8,128)(2,1)} %constant.10.clone.table_hbm.table_ref) | copy-start | bytes 786436
  68.5 18.9 %copy-start.3 = (f32[2,128]{1,0:T(2,128)S(1)}, f32[2,128]{1,0:T(2,128)}, u32[]{:S(2)}) copy-start(f32[2,128]{1,0:T(2,128)} %constant.14.clone.weight_ref) | copy-start | bytes 3076

commit v4 on v3

--- a/solution.py
+++ b/solution.py
@@ -167,7 +167,7 @@
 
 
 def finish(
-    in_ref, field_ref, table_ref, turn_ref, shell_ref, spot_ref, out_hbm, sums_ref, wide_ref, out_ref, energy_ref, sems, *, scale, bins
+    in_ref, field_ref, table_ref, turn_ref, shell_ref, spot_ref, weight_ref, out_hbm, sums_ref, wide_ref, out_ref, energy_ref, sems, *, scale, bins
 ):
     _, width_x, width_y, modes = field_ref.shape
     lane = lax.broadcasted_iota(jnp.int32, (width_y, modes), 1)
@@ -213,13 +213,15 @@
         placed = placed[:count] + placed[count : 2 * count] + placed[2 * count :]
         shifted = pltpu.roll(placed, 0, 1, stride=1, stride_axis=0)
         result = result + jnp.sum(shifted, axis=0, keepdims=True)
-    sums_ref[...] = result
+    sums_ref[...] = result * weight_ref[...]
     for copy in copies:
         copy.wait()
 
 
-def mean_up(copies_ref, weight_ref, out_ref):
-    out_ref[...] = jnp.sum(copies_ref[...].astype(F32), axis=0) * weight_ref[...]
+def add_up(copies_ref, out_ref):
+    total = jnp.sum(copies_ref[...].astype(F32), axis=0)
+    lanes = out_ref.shape[0]
+    out_ref[...] = jnp.sum(total.reshape(-1, lanes, 128), axis=0)
 
 
 def tables(modes, scale_in, scale_out):
@@ -295,6 +297,7 @@
     )(slabs.reshape(shape), near_ty, fx, near_fy)
     home = lax.all_to_all(back.reshape(devices, width_x, 128), RING, 0, 0, tiled=True)
     bins = math.ceil(math.sqrt((width_x - 1) ** 2 + 49)) + 2
+    weights = jnp.asarray((1.0 / np.maximum(shell_counts(modes), 1.0)).reshape(1, modes))
     updated, sums = pl.pallas_call(
         functools.partial(finish, scale=scale_out, bins=bins),
         out_shape=[jax.ShapeDtypeStruct(field.shape, F32), jax.ShapeDtypeStruct((1, modes), F32)],
@@ -307,14 +310,13 @@
         ],
         compiler_params=params(),
         name="finish",
-    )(home, field, z_table, turn, shell, spot)
+    )(home, field, z_table, turn, shell, spot, weights)
     lanes = modes // 128
     copies = jnp.broadcast_to(sums.reshape(1, lanes, 128).astype(BF16), (devices, lanes, 128))
     everyone = lax.all_to_all(copies, RING, 0, 0, tiled=True)
-    weights = jnp.asarray((1.0 / np.maximum(shell_counts(modes), 1.0)).reshape(lanes, 128))
     spectrum = pl.pallas_call(
-        mean_up, out_shape=jax.ShapeDtypeStruct((lanes, 128), F32), compiler_params=params(), name="mean_up"
-    )(everyone, weights)
+        add_up, out_shape=jax.ShapeDtypeStruct((lanes, 128), F32), compiler_params=params(), name="add_up"
+    )(everyone.reshape(-1, 16, 128))
     return updated, spectrum.reshape(modes)
 
 

time: 88.5 us -> 88.9 us (level)
  no operation moved by 1% of the time
where the time goes in v4:
time: 88.9 us; the launch traced here: 88.7 us
  blocking collectives  80.6 us (91%)
  Pallas kernels  6.67 us (8%)
    all_to_all x1, blocking collectives, body(): slabs = lax.all_to_all(messages, RING, 0, 0, tiled=True)  35.5 us
    all_to_all x1, blocking collectives, body(): lax.all_to_all(back.reshape(devices, width_x, 128), RING, 0, 0, tiled=True)  26.2 us
    all_to_all x1, blocking collectives, body(): everyone = lax.all_to_all(copies, RING, 0, 0, tiled=True)  18.9 us
    pallas_call x1, Pallas kernels, body(): pl.pallas_call(functools.partial(planes, chunk=128), out_shape=jax.ShapeD...  2.92 us
    pallas_call x1, Pallas kernels, body(): pl.pallas_call(functools.partial(to_slabs, scale=scale_in), in_specs=[pl....  1.83 us

profile of v4, /device:TPU:1, one launch (start us, length us, event | category | flops | bytes accessed | tf_op | source)
XLA Modules:
  0.0 88.7 jit_solution(941600097825721536)
XLA Ops:
  0.6 1.8 %to_slabs.1 = (bf16[256,8,128]{2,1,0:T(8,128)(2,1)S(1)}, f32[2,8,32,256]{3,2,1,0:T(8,128)S(1)}, f32[8,32,256]{2,1,0:T(8,128)S(1)}, bf16[4,256,256]{2,1,0:T(8,128...) custom-call(f32[2,8,32,256]{3,2,1,0:T(8,128)} %field_ref.1, ...), custom_call_target="tpu_custom_call" | custom-call | tf_op jit(solution)/shard_map/to_slabs/pallas_call | solution.py:269
  2.5 0.0 copy-start.2
  2.5 35.5 %all_to_all.15 = bf16[256,8,128]{2,1,0:T(8,128)(2,1)S(1)} all-to-all(bf16[256,8,128]{2,1,0:T(8,128)(2,1)S(1)} %get-tuple-element.10), channel_id=1, replica_groups=mesh['z_lo1'=2,'z_lo0'=2,'y1'=2,'y0'=2,'core'=2,'x1'=2,'x0'=2,'z_hi'=2] ..., dimensions={0} | all-to-all | bytes 1048576 | tf_op jit(solution)/shard_map/all_to_all | solution.py:289
  37.9 0.0 copy-done.2
  37.9 2.9 %planes.1 = bf16[4,2,2,4,2,16,128]{6,5,4,3,2,1,0:T(8,128)(2,1)S(1)} custom-call(bf16[4,2,2,4,2,16,128]{6,5,4,3,2,1,0:T(8,128)(2,1)S(1)} %bitcast.5, bf16[512,1024]{1,0:T(8,128)(2,1)S(1)} %get-tuple-element.11.ty_ref, bf16[256,512]{1,0:T(8,128)(2,1)S(1)} %copy-done.2, bf16[1024,512]{1,0:T(8,128)(2,1)S(1)} %get-tuple-element.12.fy_ref), custom_call_target="tpu_custom_call" | custom-call | tf_op jit(solution)/shard_map/planes/pallas_call | solution.py:291
  40.9 0.0 copy-start
  40.9 0.0 copy-start.1
  40.9 26.2 %all_to_all.16.in_ref = bf16[256,8,128]{2,1,0:T(8,128)(2,1)S(1)} all-to-all(bf16[256,8,128]{2,1,0:T(8,128)(2,1)S(1)} %bitcast.6), channel_id=1, replica_groups=mesh['z_lo1'=2,'z_lo0'=2,'y1'=2,'y0'=2,'core'=2,'x1'=2,'x0'=2,'z_hi'=2] ..., dimensions={0} | all-to-all | bytes 1048576 | tf_op jit(solution)/shard_map/all_to_all | solution.py:298
  67.1 0.0 copy-start.3
  67.1 0.0 copy-done
  67.1 0.0 copy-done.1
  67.1 0.7 copy-done.3
  67.8 1.3 %finish.1 = (f32[2,8,32,256]{3,2,1,0:T(8,128)}, f32[1,256]{1,0:T(1,128)S(1)}) custom-call(bf16[256,8,128]{2,1,0:T(8,128)(2,1)S(1)} %all_to_all.16.in_ref, f32[2,8,32,256]{3,2,1,0:T(8,128)S(1)} %copy-done, bf16[256,512]{1,0:T(8,128)(2,1)S(1)} %copy-done.1, f32[2,8,32,256]{3,2,1,0:T(8,128)S(1)} %get-tuple-element.13.turn_ref, ...), custom_call_target="tpu_custom_call" | custom-call | tf_op jit(solution)/shard_map/finish/pallas_call | solution.py:301
  69.1 0.1 broadcast_in_dim.2
  69.2 18.9 %all_to_all.17 = bf16[256,2,128]{2,1,0:T(2,128)(2,1)S(1)} all-to-all(bf16[256,2,128]{2,1,0:T(2,128)(2,1)S(1)} %broadcast_in_dim.2), channel_id=1, replica_groups=mesh['z_lo1'=2,'z_lo0'=2,'y1'=2,'y0'=2,'core'=2,'x1'=2,'x0'=2,'z_hi'=2] ..., dimensions={0} | all-to-all | bytes 262144 | tf_op jit(solution)/shard_map/all_to_all | solution.py:316
  88.1 0.6 add_up.1
  (1 shorter events, 0.0 us)
Async XLA Ops:
  2.5 35.5 %copy-start.2 = (bf16[256,512]{1,0:T(8,128)(2,1)S(1)}, bf16[256,512]{1,0:T(8,128)(2,1)}, u32[]{:S(2)}) copy-start(bf16[256,512]{1,0:T(8,128)(2,1)} %constant.12.clone.fx_ref) | copy-start | bytes 786436
  40.9 26.2 %copy-start = (f32[2,8,32,256]{3,2,1,0:T(8,128)S(1)}, f32[2,8,32,256]{3,2,1,0:T(8,128)}, u32[]{:S(2)}) copy-start(f32[2,8,32,256]{3,2,1,0:T(8,128)} %field_ref.1) | copy-start | bytes 1572868
  40.9 26.2 %copy-start.1 = (bf16[256,512]{1,0:T(8,128)(2,1)S(1)}, bf16[256,512]{1,0:T(8,128)(2,1)}, u32[]{:S(2)}) copy-start(bf16[256,512]{1,0:T(8,128)(2,1)} %constant.10.clone.table_hbm.table_ref) | copy-start | bytes 786436
  67.1 0.7 copy-start.3

commit v5 on v4

--- a/solution.py
+++ b/solution.py
@@ -80,10 +80,10 @@
 
 
 def to_slabs(
-    field_hbm, table_hbm, ty_hbm, fy_hbm, out_ref, turn_ref, shell_ref, spot_ref, ty_ref, fy_ref, wide_ref, field, table, sems, *, scale
+    field_hbm, table_hbm, ty_hbm, fy_hbm, weight_hbm, out_ref, turn_ref, shell_ref, spot_ref, ty_ref, fy_ref, weight_ref, wide_ref, field, table, sems, *, scale
 ):
     _, width_x, width, modes = field_hbm.shape
-    pairs = (table_hbm, table), (field_hbm, field), (ty_hbm, ty_ref), (fy_hbm, fy_ref)
+    pairs = (table_hbm, table), (field_hbm, field), (weight_hbm, weight_ref), (ty_hbm, ty_ref), (fy_hbm, fy_ref)
     copies = [pltpu.make_async_copy(source, target, sems.at[k]) for k, (source, target) in enumerate(pairs)]
     for copy in copies:
         copy.start()
@@ -108,8 +108,8 @@
         for k in range(2):
             wide_ref[pl.ds(pair + k, modes, stride=width_x), :] = product[:, 128 * k : 128 * (k + 1)]
     out_ref[...] = wide_ref[...].astype(BF16).reshape(out_ref.shape)
-    copies[2].wait()
-    copies[3].wait()
+    for copy in copies[2:]:
+        copy.wait()
 
 
 def dot(left, right):
@@ -266,9 +266,10 @@
     scale_in = 1.0 / math.sqrt(modes)
     scale_out = math.sqrt(modes) / (2 * modes)
     z_table, ty, fx, fy = tables(modes, scale_in, scale_out)
-    messages, turn, shell, spot, near_ty, near_fy = pl.pallas_call(
+    weights = jnp.asarray((1.0 / np.maximum(shell_counts(modes), 1.0)).reshape(1, modes))
+    messages, turn, shell, spot, near_ty, near_fy, near_weights = pl.pallas_call(
         functools.partial(to_slabs, scale=scale_in),
-        in_specs=[pl.BlockSpec(memory_space=pltpu.HBM)] * 4,
+        in_specs=[pl.BlockSpec(memory_space=pltpu.HBM)] * 5,
         out_shape=[
             jax.ShapeDtypeStruct((devices, width_x, 128), BF16),
             jax.ShapeDtypeStruct(field.shape, F32),
@@ -276,16 +277,17 @@
             jax.ShapeDtypeStruct((width_y // 8, modes, modes), BF16),
             jax.ShapeDtypeStruct(ty.shape, BF16),
             jax.ShapeDtypeStruct(fy.shape, BF16),
+            jax.ShapeDtypeStruct(weights.shape, F32),
         ],
         scratch_shapes=[
             pltpu.VMEM((devices * width_x, 128), F32),
             pltpu.VMEM(field.shape, F32),
             pltpu.VMEM(z_table.shape, BF16),
-            pltpu.SemaphoreType.DMA((4,)),
+            pltpu.SemaphoreType.DMA((5,)),
         ],
         compiler_params=params(),
         name="to_slabs",
-    )(in_hbm(field), in_hbm(z_table), in_hbm(ty), in_hbm(fy))
+    )(*(in_hbm(array) for array in (field, z_table, ty, fy, weights)))
     slabs = lax.all_to_all(messages, RING, 0, 0, tiled=True)
     shape = (4, 2, 2, 4, 2, 2 * width_x, 128)
     back = pl.pallas_call(
@@ -297,7 +299,6 @@
     )(slabs.reshape(shape), near_ty, fx, near_fy)
     home = lax.all_to_all(back.reshape(devices, width_x, 128), RING, 0, 0, tiled=True)
     bins = math.ceil(math.sqrt((width_x - 1) ** 2 + 49)) + 2
-    weights = jnp.asarray((1.0 / np.maximum(shell_counts(modes), 1.0)).reshape(1, modes))
     updated, sums = pl.pallas_call(
         functools.partial(finish, scale=scale_out, bins=bins),
         out_shape=[jax.ShapeDtypeStruct(field.shape, F32), jax.ShapeDtypeStruct((1, modes), F32)],
@@ -310,7 +311,7 @@
         ],
         compiler_params=params(),
         name="finish",
-    )(home, field, z_table, turn, shell, spot, weights)
+    )(home, field, z_table, turn, shell, spot, near_weights)
     lanes = modes // 128
     copies = jnp.broadcast_to(sums.reshape(1, lanes, 128).astype(BF16), (devices, lanes, 128))
     everyone = lax.all_to_all(copies, RING, 0, 0, tiled=True)

time: 88.9 us -> 88.3 us (level)
  no operation moved by 1% of the time
where the time goes in v5:
time: 88.3 us; the launch traced here: 88.1 us
  blocking collectives  80.6 us (91%)
  Pallas kernels  6.71 us (8%)
    all_to_all x1, blocking collectives, body(): slabs = lax.all_to_all(messages, RING, 0, 0, tiled=True)  35.5 us
    all_to_all x1, blocking collectives, body(): lax.all_to_all(back.reshape(devices, width_x, 128), RING, 0, 0, tiled=True)  26.2 us
    all_to_all x1, blocking collectives, body(): everyone = lax.all_to_all(copies, RING, 0, 0, tiled=True)  18.9 us
    pallas_call x1, Pallas kernels, body(): pl.pallas_call(functools.partial(planes, chunk=128), out_shape=jax.ShapeD...  2.93 us
    pallas_call x1, Pallas kernels, body(): pl.pallas_call(functools.partial(to_slabs, scale=scale_in), in_specs=[pl....  1.85 us

profile of v5, /device:TPU:1, one launch (start us, length us, event | category | flops | bytes accessed | tf_op | source)
XLA Modules:
  0.0 88.1 jit_solution(5824563417704621251)
XLA Ops:
  0.6 1.9 %to_slabs.1 = (bf16[256,8,128]{2,1,0:T(8,128)(2,1)S(1)}, f32[2,8,32,256]{3,2,1,0:T(8,128)S(1)}, f32[8,32,256]{2,1,0:T(8,128)S(1)}, bf16[4,256,256]{2,1,0:T(8,128...) custom-call(f32[2,8,32,256]{3,2,1,0:T(8,128)} %field_ref.1, ...), custom_call_target="tpu_custom_call" | custom-call | tf_op jit(solution)/shard_map/to_slabs/pallas_call | solution.py:270
  2.5 0.0 copy-start.2
  2.5 35.5 %all_to_all.15 = bf16[256,8,128]{2,1,0:T(8,128)(2,1)S(1)} all-to-all(bf16[256,8,128]{2,1,0:T(8,128)(2,1)S(1)} %get-tuple-element.11), channel_id=1, replica_groups=mesh['z_lo1'=2,'z_lo0'=2,'y1'=2,'y0'=2,'core'=2,'x1'=2,'x0'=2,'z_hi'=2] ..., dimensions={0} | all-to-all | bytes 1048576 | tf_op jit(solution)/shard_map/all_to_all | solution.py:291
  38.0 0.0 copy-done.2
  38.0 2.9 %planes.1 = bf16[4,2,2,4,2,16,128]{6,5,4,3,2,1,0:T(8,128)(2,1)S(1)} custom-call(bf16[4,2,2,4,2,16,128]{6,5,4,3,2,1,0:T(8,128)(2,1)S(1)} %bitcast.5, bf16[512,1024]{1,0:T(8,128)(2,1)S(1)} %get-tuple-element.12.ty_ref, bf16[256,512]{1,0:T(8,128)(2,1)S(1)} %copy-done.2, bf16[1024,512]{1,0:T(8,128)(2,1)S(1)} %get-tuple-element.13.fy_ref), custom_call_target="tpu_custom_call" | custom-call | tf_op jit(solution)/shard_map/planes/pallas_call | solution.py:293
  40.9 0.0 copy-start
  40.9 0.0 copy-start.1
  40.9 26.2 %all_to_all.16.in_ref = bf16[256,8,128]{2,1,0:T(8,128)(2,1)S(1)} all-to-all(bf16[256,8,128]{2,1,0:T(8,128)(2,1)S(1)} %bitcast.6), channel_id=1, replica_groups=mesh['z_lo1'=2,'z_lo0'=2,'y1'=2,'y0'=2,'core'=2,'x1'=2,'x0'=2,'z_hi'=2] ..., dimensions={0} | all-to-all | bytes 1048576 | tf_op jit(solution)/shard_map/all_to_all | solution.py:300
  67.1 0.0 copy-done
  67.1 0.0 copy-done.1
  67.1 1.3 %finish.1 = (f32[2,8,32,256]{3,2,1,0:T(8,128)}, f32[1,256]{1,0:T(1,128)S(1)}) custom-call(bf16[256,8,128]{2,1,0:T(8,128)(2,1)S(1)} %all_to_all.16.in_ref, f32[2,8,32,256]{3,2,1,0:T(8,128)S(1)} %copy-done, bf16[256,512]{1,0:T(8,128)(2,1)S(1)} %copy-done.1, f32[2,8,32,256]{3,2,1,0:T(8,128)S(1)} %get-tuple-element.14.turn_ref, ...), custom_call_target="tpu_custom_call" | custom-call | tf_op jit(solution)/shard_map/finish/pallas_call | solution.py:302
  68.5 0.1 broadcast_in_dim.2
  68.6 18.9 %all_to_all.17 = bf16[256,2,128]{2,1,0:T(2,128)(2,1)S(1)} all-to-all(bf16[256,2,128]{2,1,0:T(2,128)(2,1)S(1)} %broadcast_in_dim.2), channel_id=1, replica_groups=mesh['z_lo1'=2,'z_lo0'=2,'y1'=2,'y0'=2,'core'=2,'x1'=2,'x0'=2,'z_hi'=2] ..., dimensions={0} | all-to-all | bytes 262144 | tf_op jit(solution)/shard_map/all_to_all | solution.py:317
  87.5 0.6 add_up.1
  (1 shorter events, 0.0 us)
Async XLA Ops:
  2.5 35.5 %copy-start.2 = (bf16[256,512]{1,0:T(8,128)(2,1)S(1)}, bf16[256,512]{1,0:T(8,128)(2,1)}, u32[]{:S(2)}) copy-start(bf16[256,512]{1,0:T(8,128)(2,1)} %constant.12.clone.fx_ref) | copy-start | bytes 786436
  40.9 26.2 %copy-start = (f32[2,8,32,256]{3,2,1,0:T(8,128)S(1)}, f32[2,8,32,256]{3,2,1,0:T(8,128)}, u32[]{:S(2)}) copy-start(f32[2,8,32,256]{3,2,1,0:T(8,128)} %field_ref.1) | copy-start | bytes 1572868
  40.9 26.2 %copy-start.1 = (bf16[256,512]{1,0:T(8,128)(2,1)S(1)}, bf16[256,512]{1,0:T(8,128)(2,1)}, u32[]{:S(2)}) copy-start(bf16[256,512]{1,0:T(8,128)(2,1)} %constant.10.clone.table_hbm.table_ref) | copy-start | bytes 786436

commit v6 on v5

--- a/solution.py
+++ b/solution.py
@@ -167,17 +167,13 @@
 
 
 def finish(
-    in_ref, field_ref, table_ref, turn_ref, shell_ref, spot_ref, weight_ref, out_hbm, sums_ref, wide_ref, out_ref, energy_ref, sems, *, scale, bins
+    in_ref, field_ref, table_ref, turn_ref, shell_ref, spot_ref, weight_ref, out_ref, sums_ref, wide_ref, energy_ref, *, scale, bins
 ):
     _, width_x, width_y, modes = field_ref.shape
     lane = lax.broadcasted_iota(jnp.int32, (width_y, modes), 1)
     sign = jnp.where(lane % 2 == 0, 1.0, -1.0)
     wide_ref[...] = in_ref[...].reshape(wide_ref.shape).astype(F32)
     table = table_ref[...]
-    copies = [
-        pltpu.make_async_copy(out_ref.at[:, pl.ds(at, 1)], out_hbm.at[:, pl.ds(at, 1)], sems.at[at])
-        for at in range(width_x)
-    ]
     for at in range(width_x):
         slab = wide_ref[pl.ds(at, modes, stride=width_x), :].astype(BF16)
         got = lax.dot_general(slab, table, (((0,), (0,)), ((), ())), preferred_element_type=F32)
@@ -191,7 +187,6 @@
         new_i = v * cos - u * sin
         out_ref[0, at] = new_r
         out_ref[1, at] = new_i
-        copies[at].start()
         energy_ref[at] = new_r * new_r + new_i * new_i
     result = jnp.zeros((1, modes), F32)
     for block in range(width_y // 8):
@@ -214,8 +209,6 @@
         shifted = pltpu.roll(placed, 0, 1, stride=1, stride_axis=0)
         result = result + jnp.sum(shifted, axis=0, keepdims=True)
     sums_ref[...] = result * weight_ref[...]
-    for copy in copies:
-        copy.wait()
 
 
 def add_up(copies_ref, out_ref):
@@ -301,14 +294,8 @@
     bins = math.ceil(math.sqrt((width_x - 1) ** 2 + 49)) + 2
     updated, sums = pl.pallas_call(
         functools.partial(finish, scale=scale_out, bins=bins),
-        out_shape=[jax.ShapeDtypeStruct(field.shape, F32), jax.ShapeDtypeStruct((1, modes), F32)],
-        out_specs=[pl.BlockSpec(memory_space=pltpu.HBM), pl.BlockSpec(memory_space=pltpu.VMEM)],
-        scratch_shapes=[
-            pltpu.VMEM((devices * width_x, 128), F32),
-            pltpu.VMEM(field.shape, F32),
-            pltpu.VMEM((width_x, width_y, modes), F32),
-            pltpu.SemaphoreType.DMA((width_x,)),
-        ],
+        out_shape=[pltpu.VMEM(field.shape, F32), jax.ShapeDtypeStruct((1, modes), F32)],
+        scratch_shapes=[pltpu.VMEM((devices * width_x, 128), F32), pltpu.VMEM((width_x, width_y, modes), F32)],
         compiler_params=params(),
         name="finish",
     )(home, field, z_table, turn, shell, spot, near_weights)

time: 88.3 us -> 89 us (level)
  blocking collectives: 80.6 us -> 61.7 us
  waiting for transfers between devices: 0 us -> 11.9 us
  starting transfers between devices: 0 us -> 6.36 us
  local copies, waits for them, and re-layouts: 0.09 us -> 1.55 us
    all_to_all x1 -> x0, blocking collectives: 18.9 us -> none  [body(): everyone = lax.all_to_all(copies, RING, 0, 0, tiled=True)]
    all_to_all x0 -> x1, waiting for transfers between devices: none -> 11.9 us  [body(): everyone = lax.all_to_all(copies, RING, 0, 0, tiled=True)]
    all_to_all x0 -> x1, starting transfers between devices: none -> 6.36 us  [body(): everyone = lax.all_to_all(copies, RING, 0, 0, tiled=True)]
  transfers between devices with their start and end apart: 0 -> 1, of which waited for: 0 -> 1; matrix products, arithmetic and copies ran while one was open for 0% -> 1% of each run, Pallas kernels for 0% -> 0%
where the time goes in v6:
time: 89 us; the launch traced here: 88.7 us
  blocking collectives  61.7 us (69%)
  waiting for transfers between devices  11.9 us (13%)
  Pallas kernels  6.55 us (7%)
  starting transfers between devices  6.36 us (7%)
  local copies, waits for them, and re-layouts  1.55 us (2%)
    all_to_all x1, blocking collectives, body(): slabs = lax.all_to_all(messages, RING, 0, 0, tiled=True)  35.5 us
    all_to_all x1, blocking collectives, body(): lax.all_to_all(back.reshape(devices, width_x, 128), RING, 0, 0, tiled=True)  26.2 us
    all_to_all x1, waiting for transfers between devices, body(): everyone = lax.all_to_all(copies, RING, 0, 0, tiled=True)  11.9 us
    all_to_all x1, starting transfers between devices, body(): everyone = lax.all_to_all(copies, RING, 0, 0, tiled=True)  6.36 us
    pallas_call x1, Pallas kernels, body(): pl.pallas_call(functools.partial(planes, chunk=128), out_shape=jax.ShapeD...  2.93 us
    pallas_call x1, Pallas kernels, body(): pl.pallas_call(functools.partial(to_slabs, scale=scale_in), in_specs=[pl....  1.85 us
  transfers between devices with their start and end apart: 1, of which 1 were waited for; matrix products, arithmetic and copies ran while one was open for 1% of the time, Pallas kernels for 0%

profile of v6, /device:TPU:1, one launch (start us, length us, event | category | flops | bytes accessed | tf_op | source)
XLA Modules:
  0.0 88.7 jit_solution(13068147401634105072)
XLA Ops:
  0.6 1.9 %to_slabs.1 = (bf16[256,8,128]{2,1,0:T(8,128)(2,1)S(1)}, f32[2,8,32,256]{3,2,1,0:T(8,128)S(1)}, f32[8,32,256]{2,1,0:T(8,128)S(1)}, bf16[4,256,256]{2,1,0:T(8,128...) custom-call(f32[2,8,32,256]{3,2,1,0:T(8,128)} %field_ref.1, ...), custom_call_target="tpu_custom_call" | custom-call | tf_op jit(solution)/shard_map/to_slabs/pallas_call | solution.py:263
  2.5 0.0 copy-start.2
  2.5 35.5 %all_to_all.15 = bf16[256,8,128]{2,1,0:T(8,128)(2,1)S(1)} all-to-all(bf16[256,8,128]{2,1,0:T(8,128)(2,1)S(1)} %get-tuple-element.11), channel_id=1, replica_groups=mesh['z_lo1'=2,'z_lo0'=2,'y1'=2,'y0'=2,'core'=2,'x1'=2,'x0'=2,'z_hi'=2] ..., dimensions={0} | all-to-all | bytes 1048576 | tf_op jit(solution)/shard_map/all_to_all | solution.py:284
  38.0 0.0 copy-done.2
  38.0 2.9 %planes.1 = bf16[4,2,2,4,2,16,128]{6,5,4,3,2,1,0:T(8,128)(2,1)S(1)} custom-call(bf16[4,2,2,4,2,16,128]{6,5,4,3,2,1,0:T(8,128)(2,1)S(1)} %bitcast.5, bf16[512,1024]{1,0:T(8,128)(2,1)S(1)} %get-tuple-element.12.ty_ref, bf16[256,512]{1,0:T(8,128)(2,1)S(1)} %copy-done.2, bf16[1024,512]{1,0:T(8,128)(2,1)S(1)} %get-tuple-element.13.fy_ref), custom_call_target="tpu_custom_call" | custom-call | tf_op jit(solution)/shard_map/planes/pallas_call | solution.py:286
  40.9 0.0 copy-start
  40.9 0.0 copy-start.1
  40.9 26.2 %all_to_all.16.in_ref = bf16[256,8,128]{2,1,0:T(8,128)(2,1)S(1)} all-to-all(bf16[256,8,128]{2,1,0:T(8,128)(2,1)S(1)} %bitcast.6), channel_id=1, replica_groups=mesh['z_lo1'=2,'z_lo0'=2,'y1'=2,'y0'=2,'core'=2,'x1'=2,'x0'=2,'z_hi'=2] ..., dimensions={0} | all-to-all | bytes 1048576 | tf_op jit(solution)/shard_map/all_to_all | solution.py:293
  67.1 0.0 copy-done
  67.1 0.0 copy-done.1
  67.1 1.2 %finish.1 = (f32[2,8,32,256]{3,2,1,0:T(8,128)S(1)}, f32[1,256]{1,0:T(1,128)S(1)}) custom-call(bf16[256,8,128]{2,1,0:T(8,128)(2,1)S(1)} %all_to_all.16.in_ref, f32[2,8,32,256]{3,2,1,0:T(8,128)S(1)} %copy-done, bf16[256,512]{1,0:T(8,128)(2,1)S(1)} %copy-done.1, f32[2,8,32,256]{3,2,1,0:T(8,128)S(1)} %get-tuple-element.14.turn_ref, ...), custom_call_target="tpu_custom_call" | custom-call | tf_op jit(solution)/shard_map/finish/pallas_call | solution.py:295
  68.3 0.7 broadcast_in_dim.2
  69.1 6.4 %all-to-all-start.2 = ((bf16[256,2,128]{2,1,0:T(2,128)(2,1)}), bf16[256,2,128]{2,1,0:T(2,128)(2,1)S(1)}, u32[]{:S(2)}, u32[]{:S(2)}) async-start(bf16[256,2,128]{2,1,0:T(2,128)(2,1)} %broadcast_in_dim.2), calls=%async_computation.2 | async-start | bytes 262144 | tf_op jit(solution)/shard_map/all_to_all | solution.py:304
  75.4 0.8 copy.8
  76.2 11.9 %all-to-all-done.2 = bf16[256,2,128]{2,1,0:T(2,128)(2,1)S(1)} async-done(((bf16[256,2,128]{2,1,0:T(2,128)(2,1)}), bf16[256,2,128]{2,1,0:T(2,128)(2,1)S(1)}, u32[]{:S(2)}, u32[]{:S(2)}) %all-to-all-start.2) | async-done | bytes 131104 | tf_op jit(solution)/shard_map/all_to_all | solution.py:304
  88.1 0.6 add_up.1
  (1 shorter events, 0.0 us)
Async XLA Ops:
  2.5 35.5 %copy-start.2 = (bf16[256,512]{1,0:T(8,128)(2,1)S(1)}, bf16[256,512]{1,0:T(8,128)(2,1)}, u32[]{:S(2)}) copy-start(bf16[256,512]{1,0:T(8,128)(2,1)} %constant.12.clone.fx_ref) | copy-start | bytes 786436
  40.9 26.2 %copy-start = (f32[2,8,32,256]{3,2,1,0:T(8,128)S(1)}, f32[2,8,32,256]{3,2,1,0:T(8,128)}, u32[]{:S(2)}) copy-start(f32[2,8,32,256]{3,2,1,0:T(8,128)} %field_ref.1) | copy-start | bytes 1572868
  40.9 26.2 %copy-start.1 = (bf16[256,512]{1,0:T(8,128)(2,1)S(1)}, bf16[256,512]{1,0:T(8,128)(2,1)}, u32[]{:S(2)}) copy-start(bf16[256,512]{1,0:T(8,128)(2,1)} %constant.10.clone.table_hbm.table_ref) | copy-start | bytes 786436
  69.1 19.1 %all-to-all-start.2 = ((bf16[256,2,128]{2,1,0:T(2,128)(2,1)}), bf16[256,2,128]{2,1,0:T(2,128)(2,1)S(1)}, u32[]{:S(2)}, u32[]{:S(2)}) async-start(bf16[256,2,128]{2,1,0:T(2,128)(2,1)} %broadcast_in_dim.2), calls=%async_computation.2 | async-start | bytes 262144 | tf_op jit(solution)/shard_map/all_to_all | solution.py:304

commit v7 on v5

--- a/solution.py
+++ b/solution.py
@@ -10,9 +10,9 @@
 from jax.sharding import Mesh
 from jax.sharding import PartitionSpec as P
 
-ROW = ("z_lo1", "z_lo0", "y1", "y0", "core")
-COL = ("x1", "x0", "z_hi")
-RING = ("z_lo1", "y1", "x1", "z_hi", "z_lo0", "y0", "x0", "core")
+ROW = ("z_lo", "y", "core")
+COL = ("x", "z_hi")
+RING = ("z_hi", "z_lo", "y", "x", "core")
 
 phase_rate = 0.0002
 coupling = 0.2
@@ -28,8 +28,8 @@
 
 
 def place(width_x, width_y, modes):
-    row = functools.reduce(lambda at, axis: 2 * at + lax.axis_index(axis), ROW, 0)
-    col = functools.reduce(lambda at, axis: 2 * at + lax.axis_index(axis), COL, 0)
+    row = (lax.axis_index("z_lo") * 4 + lax.axis_index("y")) * 2 + lax.axis_index("core")
+    col = lax.axis_index("x") * 2 + lax.axis_index("z_hi")
     return row * width_x - modes // 2, col * width_y - modes // 2
 
 
@@ -80,7 +80,7 @@
 
 
 def to_slabs(
-    field_hbm, table_hbm, ty_hbm, fy_hbm, weight_hbm, out_ref, turn_ref, shell_ref, spot_ref, ty_ref, fy_ref, weight_ref, wide_ref, field, table, sems, *, scale
+    field_hbm, table_hbm, ty_hbm, fy_hbm, weight_hbm, out_ref, turn_ref, shell_ref, spot_ref, ty_ref, fy_ref, weight_ref, field, table, wide_ref, sems, *, scale
 ):
     _, width_x, width, modes = field_hbm.shape
     pairs = (table_hbm, table), (field_hbm, field), (weight_hbm, weight_ref), (ty_hbm, ty_ref), (fy_hbm, fy_ref)
@@ -138,8 +138,8 @@
     half = 64
     fx = fx_ref[...]
     tx = fx.T
-    spots = [(x1, x0, z) for x1 in range(2) for x0 in range(2) for z in range(2)]
-    blocks = [in_ref[:, x1, z, :, x0].reshape(modes, 128) for x1, x0, z in spots]
+    spots = [(x, z) for x in range(4) for z in range(2)]
+    blocks = [in_ref[z, :, x].reshape(modes, 128) for x, z in spots]
     lines = jnp.concatenate(
         [jnp.concatenate([b[:, half * plane : half * (plane + 1)] for b in blocks], axis=1) for plane in range(2)], axis=0
     )
@@ -160,10 +160,10 @@
             back_ref[mine, real] = back_x[:, :chunk]
             back_ref[mine, imag] = back_x[:, chunk:]
     done = dot(back_ref[...], fy_ref[...]).astype(BF16)
-    for k, (x1, x0, z) in enumerate(spots):
+    for k, (x, z) in enumerate(spots):
         at = slice(half * k, half * (k + 1))
         message = jnp.concatenate([done[:modes, at], done[modes:, at]], axis=1)
-        out_ref[:, x1, z, :, x0] = message.reshape(4, 4, 16, 128)
+        out_ref[z, :, x] = message.reshape(16, 16, 128)
 
 
 def finish(
@@ -238,8 +238,7 @@
     odd = low_sin.copy()
     odd[0] = cos[:, modes]
     tx = np.concatenate([low_cos, odd], axis=0)
-    bits = np.arange(modes).reshape(2, 2, 2, 2, 2, modes // 32)
-    fx = tx.T[bits.transpose(0, 2, 1, 3, 4, 5).reshape(-1)]
+    fx = tx.T
     scaled = (z_table, ty * scale_in, fx * scale_in, fy * (scale_out * scale_out / scale_in))
     return [jnp.asarray(np.ascontiguousarray(t), BF16) for t in scaled]
 
@@ -267,7 +266,7 @@
     scale_out = math.sqrt(modes) / (2 * modes)
     z_table, ty, fx, fy = tables(modes, scale_in, scale_out)
     weights = jnp.asarray((1.0 / np.maximum(shell_counts(modes), 1.0)).reshape(1, modes))
-    messages, turn, shell, spot, near_ty, near_fy, near_weights = pl.pallas_call(
+    messages, turn, shell, spot, near_ty, near_fy, near_weights, near_field, near_table = pl.pallas_call(
         functools.partial(to_slabs, scale=scale_in),
         in_specs=[pl.BlockSpec(memory_space=pltpu.HBM)] * 5,
         out_shape=[
@@ -278,18 +277,18 @@
             jax.ShapeDtypeStruct(ty.shape, BF16),
             jax.ShapeDtypeStruct(fy.shape, BF16),
             jax.ShapeDtypeStruct(weights.shape, F32),
+            jax.ShapeDtypeStruct(field.shape, F32),
+            jax.ShapeDtypeStruct(z_table.shape, BF16),
         ],
         scratch_shapes=[
             pltpu.VMEM((devices * width_x, 128), F32),
-            pltpu.VMEM(field.shape, F32),
-            pltpu.VMEM(z_table.shape, BF16),
             pltpu.SemaphoreType.DMA((5,)),
         ],
         compiler_params=params(),
         name="to_slabs",
     )(*(in_hbm(array) for array in (field, z_table, ty, fy, weights)))
     slabs = lax.all_to_all(messages, RING, 0, 0, tiled=True)
-    shape = (4, 2, 2, 4, 2, 2 * width_x, 128)
+    shape = (2, 16, 4, 2 * width_x, 128)
     back = pl.pallas_call(
         functools.partial(planes, chunk=128),
         out_shape=jax.ShapeDtypeStruct(shape, BF16),
@@ -311,7 +310,7 @@
         ],
         compiler_params=params(),
         name="finish",
-    )(home, field, z_table, turn, shell, spot, near_weights)
+    )(home, near_field, near_table, turn, shell, spot, near_weights)
     lanes = modes // 128
     copies = jnp.broadcast_to(sums.reshape(1, lanes, 128).astype(BF16), (devices, lanes, 128))
     everyone = lax.all_to_all(copies, RING, 0, 0, tiled=True)
@@ -322,7 +321,7 @@
 
 
 def solution(mesh):
-    split = Mesh(mesh.devices.reshape((2,) * 8), ROW + COL)
+    split = Mesh(mesh.devices.reshape(4, 4, 2, 4, 2), ROW + COL)
     placed = (P(None, ROW, COL, None),)
     return jax.shard_map(
         body, mesh=split, in_specs=placed, out_specs=(P(None, ROW, COL, None), P()), check_vma=False

time: 88.3 us -> 87.9 us (level)
  no operation moved by 1% of the time
where the time goes in v7:
time: 87.9 us; the launch traced here: 87.7 us
  blocking collectives  80.2 us (91%)
  Pallas kernels  6.74 us (8%)
    all_to_all x1, blocking collectives, body(): slabs = lax.all_to_all(messages, RING, 0, 0, tiled=True)  35.3 us
    all_to_all x1, blocking collectives, body(): lax.all_to_all(back.reshape(devices, width_x, 128), RING, 0, 0, tiled=True)  25.9 us
    all_to_all x1, blocking collectives, body(): everyone = lax.all_to_all(copies, RING, 0, 0, tiled=True)  19 us
    pallas_call x1, Pallas kernels, body(): pl.pallas_call(functools.partial(planes, chunk=128), out_shape=jax.ShapeD...  2.92 us
    pallas_call x1, Pallas kernels, body(): pl.pallas_call(functools.partial(to_slabs, scale=scale_in), in_specs=[pl....  1.85 us

profile of v7, /device:TPU:1, one launch (start us, length us, event | category | flops | bytes accessed | tf_op | source)
XLA Modules:
  0.0 87.7 jit_solution(5554083826394534414)
XLA Ops:
  0.6 1.9 %to_slabs.1 = (bf16[256,8,128]{2,1,0:T(8,128)(2,1)S(1)}, f32[2,8,32,256]{3,2,1,0:T(8,128)S(1)}, f32[8,32,256]{2,1,0:T(8,128)S(1)}, bf16[4,256,256]{2,1,0:T(8,128...) custom-call(f32[2,8,32,256]{3,2,1,0:T(8,128)} %field_hbm.1, ...), custom_call_target="tpu_custom_call" | custom-call | tf_op jit(solution)/shard_map/to_slabs/pallas_call | solution.py:269
  2.5 0.0 copy-start
  2.5 35.3 %all_to_all.15 = bf16[256,8,128]{2,1,0:T(8,128)(2,1)S(1)} all-to-all(bf16[256,8,128]{2,1,0:T(8,128)(2,1)S(1)} %get-tuple-element.13), channel_id=1, replica_groups=mesh['z_lo'=4,'y'=4,'core'=2,'x'=4,'z_hi'=2] {'z_hi','z_lo','y','x','core'}, dimensions={0} | all-to-all | bytes 1048576 | tf_op jit(solution)/shard_map/all_to_all | solution.py:290
  37.8 0.0 copy-done
  37.8 2.9 %planes.1 = bf16[2,16,4,16,128]{4,3,2,1,0:T(8,128)(2,1)S(1)} custom-call(bf16[2,16,4,16,128]{4,3,2,1,0:T(8,128)(2,1)S(1)} %bitcast.5, bf16[512,1024]{1,0:T(8,128)(2,1)S(1)} %get-tuple-element.14.ty_ref, bf16[256,512]{1,0:T(8,128)(2,1)S(1)} %copy-done, bf16[1024,512]{1,0:T(8,128)(2,1)S(1)} %get-tuple-element.15.fy_ref), custom_call_target="tpu_custom_call" | custom-call | tf_op jit(solution)/shard_map/planes/pallas_call | solution.py:292
  40.8 25.9 %all_to_all.16.in_ref = bf16[256,8,128]{2,1,0:T(8,128)(2,1)S(1)} all-to-all(bf16[256,8,128]{2,1,0:T(8,128)(2,1)S(1)} %bitcast.6), channel_id=1, replica_groups=mesh['z_lo'=4,'y'=4,'core'=2,'x'=4,'z_hi'=2] {'z_hi','z_lo','y','x','core'}, dimensions={0} | all-to-all | bytes 1048576 | tf_op jit(solution)/shard_map/all_to_all | solution.py:299
  66.6 1.4 %finish.1 = (f32[2,8,32,256]{3,2,1,0:T(8,128)}, f32[1,256]{1,0:T(1,128)S(1)}) custom-call(bf16[256,8,128]{2,1,0:T(8,128)(2,1)S(1)} %all_to_all.16.in_ref, f32[2,8,32,256]{3,2,1,0:T(8,128)S(1)} %get-tuple-element.16.field_ref, bf16[256,512]{1,0:T(8,128)(2,1)S(1)} %get-tuple-element.17.table_ref, f32[2,8,32,256]{3,2,1,0:T(8,128)S(1)} %get-tuple-element.18.turn_ref, ...), custom_call_target="tpu_custom_call" | custom-call | tf_op jit(solution)/shard_map/finish/pallas_call | solution.py:301
  68.0 0.1 broadcast_in_dim.2
  68.1 19.0 %all_to_all.17 = bf16[256,2,128]{2,1,0:T(2,128)(2,1)S(1)} all-to-all(bf16[256,2,128]{2,1,0:T(2,128)(2,1)S(1)} %broadcast_in_dim.2), channel_id=1, replica_groups=mesh['z_lo'=4,'y'=4,'core'=2,'x'=4,'z_hi'=2] {'z_hi','z_lo','y','x','core'}, dimensions={0} | all-to-all | bytes 262144 | tf_op jit(solution)/shard_map/all_to_all | solution.py:316
  87.1 0.6 add_up.1
  (1 shorter events, 0.0 us)
Async XLA Ops:
  2.5 35.4 %copy-start = (bf16[256,512]{1,0:T(8,128)(2,1)S(1)}, bf16[256,512]{1,0:T(8,128)(2,1)}, u32[]{:S(2)}) copy-start(bf16[256,512]{1,0:T(8,128)(2,1)} %constant.12.clone.fx_ref) | copy-start | bytes 786436

commit v8 on v7

--- a/solution.py
+++ b/solution.py
@@ -12,7 +12,7 @@
 
 ROW = ("z_lo", "y", "core")
 COL = ("x", "z_hi")
-RING = ("z_hi", "z_lo", "y", "x", "core")
+RING = ("core", "z_hi", "z_lo", "y", "x")
 
 phase_rate = 0.0002
 coupling = 0.2
@@ -139,7 +139,7 @@
     fx = fx_ref[...]
     tx = fx.T
     spots = [(x, z) for x in range(4) for z in range(2)]
-    blocks = [in_ref[z, :, x].reshape(modes, 128) for x, z in spots]
+    blocks = [in_ref[:, z, :, x].reshape(modes, 128) for x, z in spots]
     lines = jnp.concatenate(
         [jnp.concatenate([b[:, half * plane : half * (plane + 1)] for b in blocks], axis=1) for plane in range(2)], axis=0
     )
@@ -163,7 +163,7 @@
     for k, (x, z) in enumerate(spots):
         at = slice(half * k, half * (k + 1))
         message = jnp.concatenate([done[:modes, at], done[modes:, at]], axis=1)
-        out_ref[z, :, x] = message.reshape(16, 16, 128)
+        out_ref[:, z, :, x] = message.reshape(2, 16, -1, 128)
 
 
 def finish(
@@ -238,7 +238,7 @@
     odd = low_sin.copy()
     odd[0] = cos[:, modes]
     tx = np.concatenate([low_cos, odd], axis=0)
-    fx = tx.T
+    fx = tx.T[np.arange(modes).reshape(16, 2, -1).transpose(1, 0, 2).reshape(-1)]
     scaled = (z_table, ty * scale_in, fx * scale_in, fy * (scale_out * scale_out / scale_in))
     return [jnp.asarray(np.ascontiguousarray(t), BF16) for t in scaled]
 
@@ -288,7 +288,7 @@
         name="to_slabs",
     )(*(in_hbm(array) for array in (field, z_table, ty, fy, weights)))
     slabs = lax.all_to_all(messages, RING, 0, 0, tiled=True)
-    shape = (2, 16, 4, 2 * width_x, 128)
+    shape = (2, 2, 16, 4, width_x, 128)
     back = pl.pallas_call(
         functools.partial(planes, chunk=128),
         out_shape=jax.ShapeDtypeStruct(shape, BF16),

time: 87.9 us -> 88.6 us (level)
    all_to_all x1, blocking collectives: 35.3 us -> 36.5 us  [body(): slabs = lax.all_to_all(messages, RING, 0, 0, tiled=True)]
where the time goes in v8:
time: 88.6 us; the launch traced here: 88.4 us
  blocking collectives  80.9 us (91%)
  Pallas kernels  6.75 us (8%)
    all_to_all x1, blocking collectives, body(): slabs = lax.all_to_all(messages, RING, 0, 0, tiled=True)  36.5 us
    all_to_all x1, blocking collectives, body(): lax.all_to_all(back.reshape(devices, width_x, 128), RING, 0, 0, tiled=True)  26.2 us
    all_to_all x1, blocking collectives, body(): everyone = lax.all_to_all(copies, RING, 0, 0, tiled=True)  18.3 us
    pallas_call x1, Pallas kernels, body(): pl.pallas_call(functools.partial(planes, chunk=128), out_shape=jax.ShapeD...  2.94 us
    pallas_call x1, Pallas kernels, body(): pl.pallas_call(functools.partial(to_slabs, scale=scale_in), in_specs=[pl....  1.85 us

profile of v8, /device:TPU:1, one launch (start us, length us, event | category | flops | bytes accessed | tf_op | source)
XLA Modules:
  0.0 88.4 jit_solution(15111099815377765361)
XLA Ops:
  0.6 1.9 %to_slabs.1 = (bf16[256,8,128]{2,1,0:T(8,128)(2,1)S(1)}, f32[2,8,32,256]{3,2,1,0:T(8,128)S(1)}, f32[8,32,256]{2,1,0:T(8,128)S(1)}, bf16[4,256,256]{2,1,0:T(8,128...) custom-call(f32[2,8,32,256]{3,2,1,0:T(8,128)} %field_hbm.1, ...), custom_call_target="tpu_custom_call" | custom-call | tf_op jit(solution)/shard_map/to_slabs/pallas_call | solution.py:269
  2.5 0.0 copy-start
  2.5 36.5 %all_to_all.15 = bf16[256,8,128]{2,1,0:T(8,128)(2,1)S(1)} all-to-all(bf16[256,8,128]{2,1,0:T(8,128)(2,1)S(1)} %get-tuple-element.13), channel_id=1, replica_groups=mesh['z_lo'=4,'y'=4,'core'=2,'x'=4,'z_hi'=2] {'core','z_hi','z_lo','y','x'}, dimensions={0} | all-to-all | bytes 1048576 | tf_op jit(solution)/shard_map/all_to_all | solution.py:290
  39.0 0.0 copy-done
  39.0 2.9 %planes.1 = bf16[2,2,16,4,8,128]{5,4,3,2,1,0:T(8,128)(2,1)S(1)} custom-call(bf16[2,2,16,4,8,128]{5,4,3,2,1,0:T(8,128)(2,1)S(1)} %bitcast.5, bf16[512,1024]{1,0:T(8,128)(2,1)S(1)} %get-tuple-element.14.ty_ref, bf16[256,512]{1,0:T(8,128)(2,1)S(1)} %copy-done, bf16[1024,512]{1,0:T(8,128)(2,1)S(1)} %get-tuple-element.15.fy_ref), custom_call_target="tpu_custom_call" | custom-call | tf_op jit(solution)/shard_map/planes/pallas_call | solution.py:292
  41.9 26.2 %all_to_all.16.in_ref = bf16[256,8,128]{2,1,0:T(8,128)(2,1)S(1)} all-to-all(bf16[256,8,128]{2,1,0:T(8,128)(2,1)S(1)} %bitcast.6), channel_id=1, replica_groups=mesh['z_lo'=4,'y'=4,'core'=2,'x'=4,'z_hi'=2] {'core','z_hi','z_lo','y','x'}, dimensions={0} | all-to-all | bytes 1048576 | tf_op jit(solution)/shard_map/all_to_all | solution.py:299
  68.0 1.4 %finish.1 = (f32[2,8,32,256]{3,2,1,0:T(8,128)}, f32[1,256]{1,0:T(1,128)S(1)}) custom-call(bf16[256,8,128]{2,1,0:T(8,128)(2,1)S(1)} %all_to_all.16.in_ref, f32[2,8,32,256]{3,2,1,0:T(8,128)S(1)} %get-tuple-element.16.field_ref, bf16[256,512]{1,0:T(8,128)(2,1)S(1)} %get-tuple-element.17.table_ref, f32[2,8,32,256]{3,2,1,0:T(8,128)S(1)} %get-tuple-element.18.turn_ref, ...), custom_call_target="tpu_custom_call" | custom-call | tf_op jit(solution)/shard_map/finish/pallas_call | solution.py:301
  69.4 0.1 broadcast_in_dim.2
  69.5 18.3 %all_to_all.17 = bf16[256,2,128]{2,1,0:T(2,128)(2,1)S(1)} all-to-all(bf16[256,2,128]{2,1,0:T(2,128)(2,1)S(1)} %broadcast_in_dim.2), channel_id=1, replica_groups=mesh['z_lo'=4,'y'=4,'core'=2,'x'=4,'z_hi'=2] {'core','z_hi','z_lo','y','x'}, dimensions={0} | all-to-all | bytes 262144 | tf_op jit(solution)/shard_map/all_to_all | solution.py:316
  87.8 0.6 add_up.1
  (1 shorter events, 0.0 us)
Async XLA Ops:
  2.5 36.5 %copy-start = (bf16[256,512]{1,0:T(8,128)(2,1)S(1)}, bf16[256,512]{1,0:T(8,128)(2,1)}, u32[]{:S(2)}) copy-start(bf16[256,512]{1,0:T(8,128)(2,1)} %constant.12.clone.fx_ref) | copy-start | bytes 786436

commit v9 on v7

--- a/solution.py
+++ b/solution.py
@@ -143,12 +143,12 @@
     lines = jnp.concatenate(
         [jnp.concatenate([b[:, half * plane : half * (plane + 1)] for b in blocks], axis=1) for plane in range(2)], axis=0
     )
-    along_y = dot(lines, ty_ref[...]).astype(BF16)
+    along_y = [dot(lines[k * modes : (k + 1) * modes], ty_ref[...]).astype(BF16) for k in range(2)]
     for plane in range(2):
         mine = slice(plane * modes, (plane + 1) * modes)
         for start in range(0, grid, chunk):
             real, imag = slice(start, start + chunk), slice(grid + start, grid + start + chunk)
-            even_odd = dot(tx, jnp.concatenate([along_y[mine, real], along_y[mine, imag]], axis=1))
+            even_odd = dot(tx, jnp.concatenate([along_y[plane][:, real], along_y[plane][:, imag]], axis=1))
             even, odd = even_odd[:modes], even_odd[modes:]
             parts = even[:, :chunk], even[:, chunk:], odd[:, :chunk], odd[:, chunk:]
             top, rest = cube([p[:16] for p in parts], True), cube([p[16:] for p in parts], False)
@@ -213,7 +213,10 @@
         placed = placed[:count] + placed[count : 2 * count] + placed[2 * count :]
         shifted = pltpu.roll(placed, 0, 1, stride=1, stride_axis=0)
         result = result + jnp.sum(shifted, axis=0, keepdims=True)
-    sums_ref[...] = result * weight_ref[...]
+    share = result * weight_ref[...]
+    lines = [share[:, 128 * k : 128 * (k + 1)] for k in range(modes // 128)]
+    group = jnp.concatenate(lines * (16 // len(lines)), axis=0).astype(BF16)
+    sums_ref[...] = jnp.broadcast_to(group[None], sums_ref.shape)
     for copy in copies:
         copy.wait()
 
@@ -298,9 +301,10 @@
     )(slabs.reshape(shape), near_ty, fx, near_fy)
     home = lax.all_to_all(back.reshape(devices, width_x, 128), RING, 0, 0, tiled=True)
     bins = math.ceil(math.sqrt((width_x - 1) ** 2 + 49)) + 2
-    updated, sums = pl.pallas_call(
+    lanes = modes // 128
+    updated, copies = pl.pallas_call(
         functools.partial(finish, scale=scale_out, bins=bins),
-        out_shape=[jax.ShapeDtypeStruct(field.shape, F32), jax.ShapeDtypeStruct((1, modes), F32)],
+        out_shape=[jax.ShapeDtypeStruct(field.shape, F32), jax.ShapeDtypeStruct((devices * lanes // 16, 16, 128), BF16)],
         out_specs=[pl.BlockSpec(memory_space=pltpu.HBM), pl.BlockSpec(memory_space=pltpu.VMEM)],
         scratch_shapes=[
             pltpu.VMEM((devices * width_x, 128), F32),
@@ -311,9 +315,7 @@
         compiler_params=params(),
         name="finish",
     )(home, near_field, near_table, turn, shell, spot, near_weights)
-    lanes = modes // 128
-    copies = jnp.broadcast_to(sums.reshape(1, lanes, 128).astype(BF16), (devices, lanes, 128))
-    everyone = lax.all_to_all(copies, RING, 0, 0, tiled=True)
+    everyone = lax.all_to_all(copies.reshape(devices, lanes, 128), RING, 0, 0, tiled=True)
     spectrum = pl.pallas_call(
         add_up, out_shape=jax.ShapeDtypeStruct((lanes, 128), F32), compiler_params=params(), name="add_up"
     )(everyone.reshape(-1, 16, 128))

time: 87.9 us -> 87.8 us (level)
  no operation moved by 1% of the time
where the time goes in v9:
time: 87.8 us; the launch traced here: 87.6 us
  blocking collectives  80.2 us (91%)
  Pallas kernels  6.69 us (8%)
    all_to_all x1, blocking collectives, body(): slabs = lax.all_to_all(messages, RING, 0, 0, tiled=True)  35.3 us
    all_to_all x1, blocking collectives, body(): lax.all_to_all(back.reshape(devices, width_x, 128), RING, 0, 0, tiled=True)  25.9 us
    all_to_all x1, blocking collectives, body(): lax.all_to_all(copies.reshape(devices, lanes, 128), RING, 0, 0, tiled=True)  19 us
    pallas_call x1, Pallas kernels, body(): pl.pallas_call(functools.partial(planes, chunk=128), out_shape=jax.ShapeD...  2.88 us
    pallas_call x1, Pallas kernels, body(): pl.pallas_call(functools.partial(to_slabs, scale=scale_in), in_specs=[pl....  1.85 us

profile of v9, /device:TPU:1, one launch (start us, length us, event | category | flops | bytes accessed | tf_op | source)
XLA Modules:
  0.0 87.6 jit_solution(4957169455573455096)
XLA Ops:
  0.6 1.9 %to_slabs.1 = (bf16[256,8,128]{2,1,0:T(8,128)(2,1)S(1)}, f32[2,8,32,256]{3,2,1,0:T(8,128)S(1)}, f32[8,32,256]{2,1,0:T(8,128)S(1)}, bf16[4,256,256]{2,1,0:T(8,128...) custom-call(f32[2,8,32,256]{3,2,1,0:T(8,128)} %field_hbm.1, ...), custom_call_target="tpu_custom_call" | custom-call | tf_op jit(solution)/shard_map/to_slabs/pallas_call | solution.py:272
  2.5 0.0 copy-start
  2.5 35.3 %all_to_all.15 = bf16[256,8,128]{2,1,0:T(8,128)(2,1)S(1)} all-to-all(bf16[256,8,128]{2,1,0:T(8,128)(2,1)S(1)} %get-tuple-element.13), channel_id=1, replica_groups=mesh['z_lo'=4,'y'=4,'core'=2,'x'=4,'z_hi'=2] {'z_hi','z_lo','y','x','core'}, dimensions={0} | all-to-all | bytes 1048576 | tf_op jit(solution)/shard_map/all_to_all | solution.py:293
  37.8 0.0 copy-done
  37.8 2.9 %planes.1 = bf16[2,16,4,16,128]{4,3,2,1,0:T(8,128)(2,1)S(1)} custom-call(bf16[2,16,4,16,128]{4,3,2,1,0:T(8,128)(2,1)S(1)} %bitcast.5, bf16[512,1024]{1,0:T(8,128)(2,1)S(1)} %get-tuple-element.14.ty_ref, bf16[256,512]{1,0:T(8,128)(2,1)S(1)} %copy-done, bf16[1024,512]{1,0:T(8,128)(2,1)S(1)} %get-tuple-element.15.fy_ref), custom_call_target="tpu_custom_call" | custom-call | tf_op jit(solution)/shard_map/planes/pallas_call | solution.py:295
  40.7 25.9 %all_to_all.16.in_ref = bf16[256,8,128]{2,1,0:T(8,128)(2,1)S(1)} all-to-all(bf16[256,8,128]{2,1,0:T(8,128)(2,1)S(1)} %bitcast.6), channel_id=1, replica_groups=mesh['z_lo'=4,'y'=4,'core'=2,'x'=4,'z_hi'=2] {'z_hi','z_lo','y','x','core'}, dimensions={0} | all-to-all | bytes 1048576 | tf_op jit(solution)/shard_map/all_to_all | solution.py:302
  66.6 1.4 %finish.1 = (f32[2,8,32,256]{3,2,1,0:T(8,128)}, bf16[32,16,128]{2,1,0:T(8,128)(2,1)S(1)}) custom-call(bf16[256,8,128]{2,1,0:T(8,128)(2,1)S(1)} %all_to_all.16.in_ref, f32[2,8,32,256]{3,2,1,0:T(8,128)S(1)} %get-tuple-element.16.field_ref, bf16[256,512]{1,0:T(8,128)(2,1)S(1)} %get-tuple-element.17.table_ref, f32[2,8,32,256]{3,2,1,0:T(8,128)S(1)} %get-tuple-element.18.turn_ref, ...), custom_call_target="tpu_custom_call" | custom-call | tf_op jit(solution)/shard_map/finish/pallas_call | solution.py:305
  68.0 19.0 %all_to_all.17 = bf16[256,2,128]{2,1,0:T(2,128)(2,1)S(1)} all-to-all(bf16[256,2,128]{2,1,0:T(2,128)(2,1)S(1)} %bitcast.8), channel_id=1, replica_groups=mesh['z_lo'=4,'y'=4,'core'=2,'x'=4,'z_hi'=2] {'z_hi','z_lo','y','x','core'}, dimensions={0} | all-to-all | bytes 262144 | tf_op jit(solution)/shard_map/all_to_all | solution.py:318
  87.0 0.6 add_up.1
Async XLA Ops:
  2.5 35.4 %copy-start = (bf16[256,512]{1,0:T(8,128)(2,1)S(1)}, bf16[256,512]{1,0:T(8,128)(2,1)}, u32[]{:S(2)}) copy-start(bf16[256,512]{1,0:T(8,128)(2,1)} %constant.12.clone.fx_ref) | copy-start | bytes 786436

commit v10 on v7

--- a/solution.py
+++ b/solution.py
@@ -312,8 +312,10 @@
         name="finish",
     )(home, near_field, near_table, turn, shell, spot, near_weights)
     lanes = modes // 128
-    copies = jnp.broadcast_to(sums.reshape(1, lanes, 128).astype(BF16), (devices, lanes, 128))
-    everyone = lax.all_to_all(copies, RING, 0, 0, tiled=True)
+    sums = sums + lax.ppermute(sums, "core", [(0, 1), (1, 0)])
+    chips = devices // 2
+    copies = jnp.broadcast_to(sums.reshape(1, lanes, 128).astype(BF16), (chips, lanes, 128))
+    everyone = lax.all_to_all(copies, RING[:-1], 0, 0, tiled=True)
     spectrum = pl.pallas_call(
         add_up, out_shape=jax.ShapeDtypeStruct((lanes, 128), F32), compiler_params=params(), name="add_up"
     )(everyone.reshape(-1, 16, 128))

time: 87.9 us -> 87.9 us (level)
  blocking collectives: 80.2 us -> 78.4 us
  starting transfers between devices: 0 us -> 1 us
    all_to_all x1, blocking collectives: 19 us -> 17.2 us  [body(): everyone = lax.all_to_all(copies, RING[:-1], 0, 0, tiled=True)]
    ppermute x0 -> x1, starting transfers between devices: none -> 1 us  [body(): sums = sums + lax.ppermute(sums, 'core', [(0, 1), (1, 0)])]
  transfers between devices with their start and end apart: 0 -> 1, of which waited for: 0 -> 1; matrix products, arithmetic and copies ran while one was open for 0% -> 0% of each run, Pallas kernels for 0% -> 0%
where the time goes in v10:
time: 87.9 us; the launch traced here: 87.7 us
  blocking collectives  78.4 us (89%)
  Pallas kernels  6.72 us (8%)
  starting transfers between devices  1 us (1%)
    all_to_all x1, blocking collectives, body(): slabs = lax.all_to_all(messages, RING, 0, 0, tiled=True)  35.3 us
    all_to_all x1, blocking collectives, body(): lax.all_to_all(back.reshape(devices, width_x, 128), RING, 0, 0, tiled=True)  25.9 us
    all_to_all x1, blocking collectives, body(): everyone = lax.all_to_all(copies, RING[:-1], 0, 0, tiled=True)  17.2 us
    pallas_call x1, Pallas kernels, body(): pl.pallas_call(functools.partial(planes, chunk=128), out_shape=jax.ShapeD...  2.92 us
    pallas_call x1, Pallas kernels, body(): pl.pallas_call(functools.partial(to_slabs, scale=scale_in), in_specs=[pl....  1.85 us
  transfers between devices with their start and end apart: 1, of which 1 were waited for; matrix products, arithmetic and copies ran while one was open for 0% of the time, Pallas kernels for 0%

profile of v10, /device:TPU:1, one launch (start us, length us, event | category | flops | bytes accessed | tf_op | source)
XLA Modules:
  0.0 87.7 jit_solution(8912684031089517457)
XLA Ops:
  0.6 1.9 %to_slabs.1 = (bf16[256,8,128]{2,1,0:T(8,128)(2,1)S(1)}, f32[2,8,32,256]{3,2,1,0:T(8,128)S(1)}, f32[8,32,256]{2,1,0:T(8,128)S(1)}, bf16[4,256,256]{2,1,0:T(8,128...) custom-call(f32[2,8,32,256]{3,2,1,0:T(8,128)} %field_hbm.1, ...), custom_call_target="tpu_custom_call" | custom-call | tf_op jit(solution)/shard_map/to_slabs/pallas_call | solution.py:269
  2.5 0.0 copy-start
  2.5 35.3 %all_to_all.15 = bf16[256,8,128]{2,1,0:T(8,128)(2,1)S(1)} all-to-all(bf16[256,8,128]{2,1,0:T(8,128)(2,1)S(1)} %get-tuple-element.13), channel_id=1, replica_groups=mesh['z_lo'=4,'y'=4,'core'=2,'x'=4,'z_hi'=2] {'z_hi','z_lo','y','x','core'}, dimensions={0} | all-to-all | bytes 1048576 | tf_op jit(solution)/shard_map/all_to_all | solution.py:290
  37.8 0.0 copy-done
  37.8 2.9 %planes.1 = bf16[2,16,4,16,128]{4,3,2,1,0:T(8,128)(2,1)S(1)} custom-call(bf16[2,16,4,16,128]{4,3,2,1,0:T(8,128)(2,1)S(1)} %bitcast.5, bf16[512,1024]{1,0:T(8,128)(2,1)S(1)} %get-tuple-element.14.ty_ref, bf16[256,512]{1,0:T(8,128)(2,1)S(1)} %copy-done, bf16[1024,512]{1,0:T(8,128)(2,1)S(1)} %get-tuple-element.15.fy_ref), custom_call_target="tpu_custom_call" | custom-call | tf_op jit(solution)/shard_map/planes/pallas_call | solution.py:292
  40.8 25.9 %all_to_all.16.in_ref = bf16[256,8,128]{2,1,0:T(8,128)(2,1)S(1)} all-to-all(bf16[256,8,128]{2,1,0:T(8,128)(2,1)S(1)} %bitcast.6), channel_id=1, replica_groups=mesh['z_lo'=4,'y'=4,'core'=2,'x'=4,'z_hi'=2] {'z_hi','z_lo','y','x','core'}, dimensions={0} | all-to-all | bytes 1048576 | tf_op jit(solution)/shard_map/all_to_all | solution.py:299
  66.6 1.4 %finish.1 = (f32[2,8,32,256]{3,2,1,0:T(8,128)}, f32[1,256]{1,0:T(1,128)S(1)}) custom-call(bf16[256,8,128]{2,1,0:T(8,128)(2,1)S(1)} %all_to_all.16.in_ref, f32[2,8,32,256]{3,2,1,0:T(8,128)S(1)} %get-tuple-element.16.field_ref, bf16[256,512]{1,0:T(8,128)(2,1)S(1)} %get-tuple-element.17.table_ref, f32[2,8,32,256]{3,2,1,0:T(8,128)S(1)} %get-tuple-element.18.turn_ref, ...), custom_call_target="tpu_custom_call" | custom-call | tf_op jit(solution)/shard_map/finish/pallas_call | solution.py:301
  68.0 1.0 %collective-permute-start = (f32[1,256]{1,0:T(1,128)S(1)}, f32[1,256]{1,0:T(1,128)S(1)}, u32[]{:S(2)}, u32[]{:S(2)}) collective-permute-start(f32[1,256]{1,0:T(1,128)S(1)} %get-tuple-element.23), channel_id=1, source_target_pairs={{0,8},{8,0},{1,9},{9,1},{2,10},{10,2},{3,11},{11,3},{4,12},{12,4},... | collective-permute-start | bytes 3080 | tf_op jit(solution)/shard_map/ppermute | solution.py:315
  69.0 0.8 collective-permute-done
  69.9 17.2 %all_to_all.17 = bf16[128,2,128]{2,1,0:T(2,128)(2,1)S(1)} all-to-all(bf16[128,2,128]{2,1,0:T(2,128)(2,1)S(1)} %broadcast_in_dim.2), channel_id=1, replica_groups=mesh['z_lo'=4,'y'=4,'core'=2,'x'=4,'z_hi'=2] {'z_hi','z_lo','y','x'}, dimensions={0} | all-to-all | bytes 131072 | tf_op jit(solution)/shard_map/all_to_all | solution.py:318
  87.1 0.6 add_up.1
  (2 shorter events, 0.1 us)
Async XLA Ops:
  2.5 35.4 %copy-start = (bf16[256,512]{1,0:T(8,128)(2,1)S(1)}, bf16[256,512]{1,0:T(8,128)(2,1)}, u32[]{:S(2)}) copy-start(bf16[256,512]{1,0:T(8,128)(2,1)} %constant.12.clone.fx_ref) | copy-start | bytes 786436
  68.0 1.8 %collective-permute-start = (f32[1,256]{1,0:T(1,128)S(1)}, f32[1,256]{1,0:T(1,128)S(1)}, u32[]{:S(2)}, u32[]{:S(2)}) collective-permute-start(f32[1,256]{1,0:T(1,128)S(1)} %get-tuple-element.23), channel_id=1, source_target_pairs={{0,8},{8,0},{1,9},{9,1},{2,10},{10,2},{3,11},{11,3},{4,12},{12,4},... | collective-permute-start | bytes 3080 | tf_op jit(solution)/shard_map/ppermute | solution.py:315

commit v11 on v10

--- a/solution.py
+++ b/solution.py
@@ -167,17 +167,13 @@
 
 
 def finish(
-    in_ref, field_ref, table_ref, turn_ref, shell_ref, spot_ref, weight_ref, out_hbm, sums_ref, wide_ref, out_ref, energy_ref, sems, *, scale, bins
+    in_ref, field_ref, table_ref, turn_ref, shell_ref, spot_ref, weight_ref, out_ref, sums_ref, wide_ref, energy_ref, *, scale, bins
 ):
     _, width_x, width_y, modes = field_ref.shape
     lane = lax.broadcasted_iota(jnp.int32, (width_y, modes), 1)
     sign = jnp.where(lane % 2 == 0, 1.0, -1.0)
     wide_ref[...] = in_ref[...].reshape(wide_ref.shape).astype(F32)
     table = table_ref[...]
-    copies = [
-        pltpu.make_async_copy(out_ref.at[:, pl.ds(at, 1)], out_hbm.at[:, pl.ds(at, 1)], sems.at[at])
-        for at in range(width_x)
-    ]
     for at in range(width_x):
         slab = wide_ref[pl.ds(at, modes, stride=width_x), :].astype(BF16)
         got = lax.dot_general(slab, table, (((0,), (0,)), ((), ())), preferred_element_type=F32)
@@ -191,7 +187,6 @@
         new_i = v * cos - u * sin
         out_ref[0, at] = new_r
         out_ref[1, at] = new_i
-        copies[at].start()
         energy_ref[at] = new_r * new_r + new_i * new_i
     result = jnp.zeros((1, modes), F32)
     for block in range(width_y // 8):
@@ -214,8 +209,13 @@
         shifted = pltpu.roll(placed, 0, 1, stride=1, stride_axis=0)
         result = result + jnp.sum(shifted, axis=0, keepdims=True)
     sums_ref[...] = result * weight_ref[...]
-    for copy in copies:
-        copy.wait()
+
+
+def put_out(kept_ref, sums_ref, out_hbm, same_ref, sem):
+    copy = pltpu.make_async_copy(kept_ref, out_hbm, sem)
+    copy.start()
+    same_ref[...] = sums_ref[...]
+    copy.wait()
 
 
 def add_up(copies_ref, out_ref):
@@ -298,21 +298,25 @@
     )(slabs.reshape(shape), near_ty, fx, near_fy)
     home = lax.all_to_all(back.reshape(devices, width_x, 128), RING, 0, 0, tiled=True)
     bins = math.ceil(math.sqrt((width_x - 1) ** 2 + 49)) + 2
-    updated, sums = pl.pallas_call(
+    kept, sums = pl.pallas_call(
         functools.partial(finish, scale=scale_out, bins=bins),
-        out_shape=[jax.ShapeDtypeStruct(field.shape, F32), jax.ShapeDtypeStruct((1, modes), F32)],
-        out_specs=[pl.BlockSpec(memory_space=pltpu.HBM), pl.BlockSpec(memory_space=pltpu.VMEM)],
-        scratch_shapes=[
-            pltpu.VMEM((devices * width_x, 128), F32),
-            pltpu.VMEM(field.shape, F32),
-            pltpu.VMEM((width_x, width_y, modes), F32),
-            pltpu.SemaphoreType.DMA((width_x,)),
-        ],
+        out_shape=[pltpu.VMEM(field.shape, F32), jax.ShapeDtypeStruct((1, modes), F32)],
+        scratch_shapes=[pltpu.VMEM((devices * width_x, 128), F32), pltpu.VMEM((width_x, width_y, modes), F32)],
         compiler_params=params(),
         name="finish",
     )(home, near_field, near_table, turn, shell, spot, near_weights)
     lanes = modes // 128
-    sums = sums + lax.ppermute(sums, "core", [(0, 1), (1, 0)])
+    other = lax.ppermute(sums, "core", [(0, 1), (1, 0)])
+    updated, same = pl.pallas_call(
+        put_out,
+        in_specs=[pl.BlockSpec(memory_space=pltpu.VMEM)] * 2,
+        out_shape=[jax.ShapeDtypeStruct(field.shape, F32), jax.ShapeDtypeStruct(sums.shape, F32)],
+        out_specs=[pl.BlockSpec(memory_space=pltpu.HBM), pl.BlockSpec(memory_space=pltpu.VMEM)],
+        scratch_shapes=[pltpu.SemaphoreType.DMA(())],
+        compiler_params=params(),
+        name="put_out",
+    )(kept, sums)
+    sums = same + other
     chips = devices // 2
     copies = jnp.broadcast_to(sums.reshape(1, lanes, 128).astype(BF16), (chips, lanes, 128))
     everyone = lax.all_to_all(copies, RING[:-1], 0, 0, tiled=True)

time: 87.9 us -> 87.7 us (level)
  transfers between devices with their start and end apart: 1 -> 1, of which waited for: 1 -> 0; matrix products, arithmetic and copies ran while one was open for 0% -> 0% of each run, Pallas kernels for 0% -> 1%
where the time goes in v11:
time: 87.7 us; the launch traced here: 87.5 us
  blocking collectives  78.4 us (89%)
  Pallas kernels  7.36 us (8%)
  starting transfers between devices  1 us (1%)
    all_to_all x1, blocking collectives, body(): slabs = lax.all_to_all(messages, RING, 0, 0, tiled=True)  35.3 us
    all_to_all x1, blocking collectives, body(): lax.all_to_all(back.reshape(devices, width_x, 128), RING, 0, 0, tiled=True)  25.9 us
    all_to_all x1, blocking collectives, body(): everyone = lax.all_to_all(copies, RING[:-1], 0, 0, tiled=True)  17.2 us
    pallas_call x1, Pallas kernels, body(): pl.pallas_call(functools.partial(planes, chunk=128), out_shape=jax.ShapeD...  2.92 us
    pallas_call x1, Pallas kernels, body(): pl.pallas_call(functools.partial(to_slabs, scale=scale_in), in_specs=[pl....  1.85 us
  transfers between devices with their start and end apart: 1, of which 0 were waited for; matrix products, arithmetic and copies ran while one was open for 0% of the time, Pallas kernels for 1%

profile of v11, /device:TPU:1, one launch (start us, length us, event | category | flops | bytes accessed | tf_op | source)
XLA Modules:
  0.0 87.5 jit_solution(10885638928638562872)
XLA Ops:
  0.6 1.9 %to_slabs.1 = (bf16[256,8,128]{2,1,0:T(8,128)(2,1)S(1)}, f32[2,8,32,256]{3,2,1,0:T(8,128)S(1)}, f32[8,32,256]{2,1,0:T(8,128)S(1)}, bf16[4,256,256]{2,1,0:T(8,128...) custom-call(f32[2,8,32,256]{3,2,1,0:T(8,128)} %field_hbm.1, ...), custom_call_target="tpu_custom_call" | custom-call | tf_op jit(solution)/shard_map/to_slabs/pallas_call | solution.py:269
  2.5 0.0 copy-start
  2.5 35.3 %all_to_all.15 = bf16[256,8,128]{2,1,0:T(8,128)(2,1)S(1)} all-to-all(bf16[256,8,128]{2,1,0:T(8,128)(2,1)S(1)} %get-tuple-element.15), channel_id=1, replica_groups=mesh['z_lo'=4,'y'=4,'core'=2,'x'=4,'z_hi'=2] {'z_hi','z_lo','y','x','core'}, dimensions={0} | all-to-all | bytes 1048576 | tf_op jit(solution)/shard_map/all_to_all | solution.py:290
  37.8 0.0 copy-done
  37.8 2.9 %planes.1 = bf16[2,16,4,16,128]{4,3,2,1,0:T(8,128)(2,1)S(1)} custom-call(bf16[2,16,4,16,128]{4,3,2,1,0:T(8,128)(2,1)S(1)} %bitcast.5, bf16[512,1024]{1,0:T(8,128)(2,1)S(1)} %get-tuple-element.16.ty_ref, bf16[256,512]{1,0:T(8,128)(2,1)S(1)} %copy-done, bf16[1024,512]{1,0:T(8,128)(2,1)S(1)} %get-tuple-element.17.fy_ref), custom_call_target="tpu_custom_call" | custom-call | tf_op jit(solution)/shard_map/planes/pallas_call | solution.py:292
  40.8 25.9 %all_to_all.16.in_ref = bf16[256,8,128]{2,1,0:T(8,128)(2,1)S(1)} all-to-all(bf16[256,8,128]{2,1,0:T(8,128)(2,1)S(1)} %bitcast.6), channel_id=1, replica_groups=mesh['z_lo'=4,'y'=4,'core'=2,'x'=4,'z_hi'=2] {'z_hi','z_lo','y','x','core'}, dimensions={0} | all-to-all | bytes 1048576 | tf_op jit(solution)/shard_map/all_to_all | solution.py:299
  66.6 1.2 %finish.1 = (f32[2,8,32,256]{3,2,1,0:T(8,128)S(1)}, f32[1,256]{1,0:T(1,128)S(1)}) custom-call(bf16[256,8,128]{2,1,0:T(8,128)(2,1)S(1)} %all_to_all.16.in_ref, f32[2,8,32,256]{3,2,1,0:T(8,128)S(1)} %get-tuple-element.18.field_ref, bf16[256,512]{1,0:T(8,128)(2,1)S(1)} %get-tuple-element.19.table_ref, f32[2,8,32,256]{3,2,1,0:T(8,128)S(1)} %get-tuple-element.20.turn_ref, ...), custom_call_target="tpu_custom_call" | custom-call | tf_op jit(solution)/shard_map/finish/pallas_call | solution.py:301
  67.9 1.0 %collective-permute-start = (f32[1,256]{1,0:T(1,128)S(1)}, f32[1,256]{1,0:T(1,128)S(1)}, u32[]{:S(2)}, u32[]{:S(2)}) collective-permute-start(f32[1,256]{1,0:T(1,128)S(1)} %get-tuple-element.25.sums_ref), channel_id=1, source_target_pairs={{0,8},{8,0},{1,9},{9,1},{2,10},{10,2},{3,11},{11,3},{4,12},{12,4},... | collective-permute-start | bytes 3080 | tf_op jit(solution)/shard_map/ppermute | solution.py:309
  68.9 0.8 put_out.1
  69.7 0.0 collective-permute-done
  69.7 17.2 %all_to_all.17 = bf16[128,2,128]{2,1,0:T(2,128)(2,1)S(1)} all-to-all(bf16[128,2,128]{2,1,0:T(2,128)(2,1)S(1)} %broadcast_in_dim.2), channel_id=1, replica_groups=mesh['z_lo'=4,'y'=4,'core'=2,'x'=4,'z_hi'=2] {'z_hi','z_lo','y','x'}, dimensions={0} | all-to-all | bytes 131072 | tf_op jit(solution)/shard_map/all_to_all | solution.py:322
  86.9 0.6 add_up.1
  (2 shorter events, 0.1 us)
Async XLA Ops:
  2.5 35.4 %copy-start = (bf16[256,512]{1,0:T(8,128)(2,1)S(1)}, bf16[256,512]{1,0:T(8,128)(2,1)}, u32[]{:S(2)}) copy-start(bf16[256,512]{1,0:T(8,128)(2,1)} %constant.12.clone.fx_ref) | copy-start | bytes 786436
  67.9 1.8 %collective-permute-start = (f32[1,256]{1,0:T(1,128)S(1)}, f32[1,256]{1,0:T(1,128)S(1)}, u32[]{:S(2)}, u32[]{:S(2)}) collective-permute-start(f32[1,256]{1,0:T(1,128)S(1)} %get-tuple-element.25.sums_ref), channel_id=1, source_target_pairs={{0,8},{8,0},{1,9},{9,1},{2,10},{10,2},{3,11},{11,3},{4,12},{12,4},... | collective-permute-start | bytes 3080 | tf_op jit(solution)/shard_map/ppermute | solution.py:309

commit v12 on v11

--- a/solution.py
+++ b/solution.py
@@ -143,12 +143,12 @@
     lines = jnp.concatenate(
         [jnp.concatenate([b[:, half * plane : half * (plane + 1)] for b in blocks], axis=1) for plane in range(2)], axis=0
     )
-    along_y = dot(lines, ty_ref[...]).astype(BF16)
+    along_y = [dot(lines[k * modes : (k + 1) * modes], ty_ref[...]).astype(BF16) for k in range(2)]
     for plane in range(2):
         mine = slice(plane * modes, (plane + 1) * modes)
         for start in range(0, grid, chunk):
             real, imag = slice(start, start + chunk), slice(grid + start, grid + start + chunk)
-            even_odd = dot(tx, jnp.concatenate([along_y[mine, real], along_y[mine, imag]], axis=1))
+            even_odd = dot(tx, jnp.concatenate([along_y[plane][:, real], along_y[plane][:, imag]], axis=1))
             even, odd = even_odd[:modes], even_odd[modes:]
             parts = even[:, :chunk], even[:, chunk:], odd[:, :chunk], odd[:, chunk:]
             top, rest = cube([p[:16] for p in parts], True), cube([p[16:] for p in parts], False)

time: 87.7 us -> 87.7 us (level)
  no operation moved by 1% of the time
where the time goes in v12:
time: 87.7 us; the launch traced here: 87.5 us
  blocking collectives  78.4 us (89%)
  Pallas kernels  7.32 us (8%)
  starting transfers between devices  1 us (1%)
    all_to_all x1, blocking collectives, body(): slabs = lax.all_to_all(messages, RING, 0, 0, tiled=True)  35.3 us
    all_to_all x1, blocking collectives, body(): lax.all_to_all(back.reshape(devices, width_x, 128), RING, 0, 0, tiled=True)  25.9 us
    all_to_all x1, blocking collectives, body(): everyone = lax.all_to_all(copies, RING[:-1], 0, 0, tiled=True)  17.2 us
    pallas_call x1, Pallas kernels, body(): pl.pallas_call(functools.partial(planes, chunk=128), out_shape=jax.ShapeD...  2.88 us
    pallas_call x1, Pallas kernels, body(): pl.pallas_call(functools.partial(to_slabs, scale=scale_in), in_specs=[pl....  1.85 us
  transfers between devices with their start and end apart: 1, of which 0 were waited for; matrix products, arithmetic and copies ran while one was open for 0% of the time, Pallas kernels for 1%

profile of v12, /device:TPU:1, one launch (start us, length us, event | category | flops | bytes accessed | tf_op | source)
XLA Modules:
  0.0 87.5 jit_solution(8497090622955506153)
XLA Ops:
  0.6 1.9 %to_slabs.1 = (bf16[256,8,128]{2,1,0:T(8,128)(2,1)S(1)}, f32[2,8,32,256]{3,2,1,0:T(8,128)S(1)}, f32[8,32,256]{2,1,0:T(8,128)S(1)}, bf16[4,256,256]{2,1,0:T(8,128...) custom-call(f32[2,8,32,256]{3,2,1,0:T(8,128)} %field_hbm.1, ...), custom_call_target="tpu_custom_call" | custom-call | tf_op jit(solution)/shard_map/to_slabs/pallas_call | solution.py:269
  2.5 0.0 copy-start
  2.5 35.3 %all_to_all.15 = bf16[256,8,128]{2,1,0:T(8,128)(2,1)S(1)} all-to-all(bf16[256,8,128]{2,1,0:T(8,128)(2,1)S(1)} %get-tuple-element.15), channel_id=1, replica_groups=mesh['z_lo'=4,'y'=4,'core'=2,'x'=4,'z_hi'=2] {'z_hi','z_lo','y','x','core'}, dimensions={0} | all-to-all | bytes 1048576 | tf_op jit(solution)/shard_map/all_to_all | solution.py:290
  37.8 0.0 copy-done
  37.8 2.9 %planes.1 = bf16[2,16,4,16,128]{4,3,2,1,0:T(8,128)(2,1)S(1)} custom-call(bf16[2,16,4,16,128]{4,3,2,1,0:T(8,128)(2,1)S(1)} %bitcast.5, bf16[512,1024]{1,0:T(8,128)(2,1)S(1)} %get-tuple-element.16.ty_ref, bf16[256,512]{1,0:T(8,128)(2,1)S(1)} %copy-done, bf16[1024,512]{1,0:T(8,128)(2,1)S(1)} %get-tuple-element.17.fy_ref), custom_call_target="tpu_custom_call" | custom-call | tf_op jit(solution)/shard_map/planes/pallas_call | solution.py:292
  40.7 25.9 %all_to_all.16.in_ref = bf16[256,8,128]{2,1,0:T(8,128)(2,1)S(1)} all-to-all(bf16[256,8,128]{2,1,0:T(8,128)(2,1)S(1)} %bitcast.6), channel_id=1, replica_groups=mesh['z_lo'=4,'y'=4,'core'=2,'x'=4,'z_hi'=2] {'z_hi','z_lo','y','x','core'}, dimensions={0} | all-to-all | bytes 1048576 | tf_op jit(solution)/shard_map/all_to_all | solution.py:299
  66.6 1.2 %finish.1 = (f32[2,8,32,256]{3,2,1,0:T(8,128)S(1)}, f32[1,256]{1,0:T(1,128)S(1)}) custom-call(bf16[256,8,128]{2,1,0:T(8,128)(2,1)S(1)} %all_to_all.16.in_ref, f32[2,8,32,256]{3,2,1,0:T(8,128)S(1)} %get-tuple-element.18.field_ref, bf16[256,512]{1,0:T(8,128)(2,1)S(1)} %get-tuple-element.19.table_ref, f32[2,8,32,256]{3,2,1,0:T(8,128)S(1)} %get-tuple-element.20.turn_ref, ...), custom_call_target="tpu_custom_call" | custom-call | tf_op jit(solution)/shard_map/finish/pallas_call | solution.py:301
  67.8 1.0 %collective-permute-start = (f32[1,256]{1,0:T(1,128)S(1)}, f32[1,256]{1,0:T(1,128)S(1)}, u32[]{:S(2)}, u32[]{:S(2)}) collective-permute-start(f32[1,256]{1,0:T(1,128)S(1)} %get-tuple-element.25.sums_ref), channel_id=1, source_target_pairs={{0,8},{8,0},{1,9},{9,1},{2,10},{10,2},{3,11},{11,3},{4,12},{12,4},... | collective-permute-start | bytes 3080 | tf_op jit(solution)/shard_map/ppermute | solution.py:309
  68.8 0.8 put_out.1
  69.6 0.0 collective-permute-done
  69.7 17.2 %all_to_all.17 = bf16[128,2,128]{2,1,0:T(2,128)(2,1)S(1)} all-to-all(bf16[128,2,128]{2,1,0:T(2,128)(2,1)S(1)} %broadcast_in_dim.2), channel_id=1, replica_groups=mesh['z_lo'=4,'y'=4,'core'=2,'x'=4,'z_hi'=2] {'z_hi','z_lo','y','x'}, dimensions={0} | all-to-all | bytes 131072 | tf_op jit(solution)/shard_map/all_to_all | solution.py:322
  86.9 0.6 add_up.1
  (2 shorter events, 0.1 us)
Async XLA Ops:
  2.5 35.4 %copy-start = (bf16[256,512]{1,0:T(8,128)(2,1)S(1)}, bf16[256,512]{1,0:T(8,128)(2,1)}, u32[]{:S(2)}) copy-start(bf16[256,512]{1,0:T(8,128)(2,1)} %constant.12.clone.fx_ref) | copy-start | bytes 786436
  67.8 1.8 %collective-permute-start = (f32[1,256]{1,0:T(1,128)S(1)}, f32[1,256]{1,0:T(1,128)S(1)}, u32[]{:S(2)}, u32[]{:S(2)}) collective-permute-start(f32[1,256]{1,0:T(1,128)S(1)} %get-tuple-element.25.sums_ref), channel_id=1, source_target_pairs={{0,8},{8,0},{1,9},{9,1},{2,10},{10,2},{3,11},{11,3},{4,12},{12,4},... | collective-permute-start | bytes 3080 | tf_op jit(solution)/shard_map/ppermute | solution.py:309
